TPU v7x, 256 devices: a whole 4x4x8 slice. The times are simulated.
256 devices in a mesh: sector: 16 (over y, x), obl: 16 (over z, core).
Axes of the slice: x: 4, y: 4, z: 8, core: 2. Of those that a mesh axis runs over, the one named last changes fastest.
Arguments:
- spectrum: float32 [2, 8, 32, 65536], P(None, None, 'sector', 'obl'), may hold values from -6 to 6
- quantile_index: int32 [8], replicated, may hold values from 32768 to 64512
- bands: int32 [1048576], P(('sector', 'obl')), may hold values from 1 to 1024
- default_prob: float32 [1048576], P(('sector', 'obl')), may hold values from 0.002 to 0.1
- weights: int32 [32, 1048576], P(None, ('sector', 'obl')), may hold values from 0 to 8
- live_rows: int32 [16, 16], P('sector', 'obl'), may hold values from 1 to 4096, as said below
Outputs:
- obligor_contrib: float32 [8, 1048576], P(None, ('sector', 'obl'))
- sector_share: float32 [8, 32], P(None, 'sector')
Inputs may be any that keep to these rules, and one draw needn't show every extreme that they name: `live_rows`: in each row (the devices of one sector index), the entries sum to 16384; exactly one of them equals 4096.
All inputs are finite; a program needn't handle non-finite values.
Results may differ from a plain program's by a relative error of at most 0.00011.
Values sent between devices are 32-bit elements; how exact they have to be, the bound alone decides.
No kernel may reach another device: no remote copies, remote signals or barrier semaphores. Data moves between devices by JAX's collectives and lax.ppermute only.
A program may use at most 64 MiB of HBM per device.

v0:
```python
import math

import jax
import jax.numpy as jnp
from jax import lax
from jax.sharding import PartitionSpec as P

RAD = 256
BANDS = 1024
OBL_DEV = 1024


def sent_to_all(value, axis):
    peers = lax.axis_size(axis)
    return lax.all_to_all(
        jnp.broadcast_to(value[None], (peers, *value.shape)), axis, 0, 0, tiled=True
    )


def laid_out(blocks, dim):
    lengths = list(blocks.shape[1:])
    lengths[dim] *= blocks.shape[0]
    return jnp.moveaxis(blocks, 0, dim).reshape(lengths)


def gather_directly(value, axis, dim):
    blocks = sent_to_all(value, axis)
    return laid_out(blocks, dim)


def cut_along(value, dim, peers):
    lengths = value.shape
    blocks = value.reshape(*lengths[:dim], peers, lengths[dim] // peers, *lengths[dim + 1 :])
    return jnp.moveaxis(blocks, dim, 0)


def summed_on_arrival(value, axis, dim):
    peers = lax.axis_size(axis)
    blocks = lax.all_to_all(cut_along(value, dim, peers), axis, 0, 0, tiled=True)
    return jnp.sum(blocks, axis=0)


def taken_together(value, axis):
    return sent_to_all(value, axis).sum(axis=0)


def phase_tables(rows_index, cols_index, radix):
    angle = (rows_index[:, None] * cols_index[None, :] % radix).astype(jnp.float32) * (
        2.0 * math.pi / radix
    )
    return (jnp.cos(angle), jnp.sin(angle))


def first_section(real_part, imag_part, rows_index, cols_index, radix):
    cosine, sine_table = phase_tables(rows_index, cols_index, radix)
    highest = lax.Precision.HIGHEST
    out_real = jnp.einsum("kab,ac->ckb", real_part, cosine, precision=highest) - jnp.einsum(
        "kab,ac->ckb", imag_part, sine_table, precision=highest
    )
    out_imag = jnp.einsum("kab,ac->ckb", real_part, sine_table, precision=highest) + jnp.einsum(
        "kab,ac->ckb", imag_part, cosine, precision=highest
    )
    return (out_real, out_imag)


def second_section(first_real, first_imag, cols_index, radix):
    grid_size = radix * radix
    b_index = jnp.arange(radix, dtype=jnp.int32)
    twist = (cols_index[:, None] * b_index[None, :]).astype(jnp.float32) * (
        2.0 * math.pi / grid_size
    )
    twist_cos = jnp.cos(twist)[:, None, :]
    twist_sin = jnp.sin(twist)[:, None, :]
    turned_real = first_real * twist_cos - first_imag * twist_sin
    turned_imag = first_real * twist_sin + first_imag * twist_cos
    cosine, sine_table = phase_tables(b_index, b_index, radix)
    highest = lax.Precision.HIGHEST
    loss_field = jnp.einsum("ckb,bd->kdc", turned_real, cosine, precision=highest) - jnp.einsum(
        "ckb,bd->kdc", turned_imag, sine_table, precision=highest
    )
    return loss_field / grid_size


def whole_rows(loss_field, quantiles, band_count):
    grid_size = loss_field.shape[1]
    positions = jnp.arange(grid_size, dtype=jnp.int32)
    upper_tail = jnp.sum(
        jnp.where(positions[None, :] >= quantiles[:, None], loss_field, 0.0), axis=1
    )
    index_table = (quantiles - band_count)[:, None] + jnp.arange(band_count, dtype=jnp.int32)[
        None, :
    ]
    window = jnp.take_along_axis(loss_field, index_table, axis=1)
    return (upper_tail, window)


def tail_lookup(all_tables, scaled, band_rows):
    scen_count, sectors_all, band_count = all_tables.shape
    row_total = band_rows.shape[0]
    block_size = math.gcd(row_total, 512)
    flat_tables = all_tables.reshape(scen_count * sectors_all, band_count)
    band_offsets = jnp.arange(band_count, dtype=jnp.int32)
    highest = lax.Precision.HIGHEST

    def block_step(block_turn, running):
        contrib, partial_value = running
        block_start = block_turn * block_size
        band_block = lax.dynamic_slice_in_dim(band_rows, block_start, block_size, 0)
        scaled_block = lax.dynamic_slice_in_dim(scaled, block_start, block_size, 1)
        one_hot = (band_offsets[:, None] == band_block[None, :]).astype(jnp.float32)
        looked = jnp.dot(flat_tables, one_hot, precision=highest).reshape(
            scen_count, sectors_all, block_size
        )
        product = scaled_block[None, :, :] * looked
        contrib = lax.dynamic_update_slice_in_dim(contrib, jnp.sum(product, axis=1), block_start, 1)
        return (contrib, partial_value + jnp.sum(product, axis=2))

    initial = (
        jnp.zeros((scen_count, row_total), jnp.float32),
        jnp.zeros((scen_count, sectors_all), jnp.float32),
    )
    return lax.fori_loop(0, row_total // block_size, block_step, initial)


def on_device(spectrum, quantile_index, bands, default_prob, weights, live_rows):
    scen_count = spectrum.shape[1]
    sec_local = spectrum.shape[2]
    batch_rows = scen_count * sec_local
    radix = RAD
    grid_size = radix * radix
    obl_count = lax.axis_size("obl")
    quantiles = jnp.repeat(quantile_index, sec_local)
    band_offsets = jnp.arange(BANDS, dtype=jnp.int32)
    highest = lax.Precision.HIGHEST
    upper_tri = (band_offsets[:, None] + band_offsets[None, :] >= BANDS - 1).astype(jnp.float32)
    full_index = jnp.arange(radix, dtype=jnp.int32)
    flat_spectra = spectrum.reshape(2, batch_rows, grid_size // obl_count)
    mine = lax.all_to_all(flat_spectra, "obl", split_axis=1, concat_axis=2, tiled=True)
    my_rows = batch_rows // obl_count
    mine = mine.reshape(2, my_rows, radix, radix)
    first_real, first_imag = first_section(mine[0], mine[1], full_index, full_index, radix)
    loss_field = second_section(first_real, first_imag, full_index, radix).reshape(
        my_rows, grid_size
    )
    my_quantiles = lax.dynamic_slice_in_dim(quantiles, lax.axis_index("obl") * my_rows, my_rows, 0)
    upper_tail, window = whole_rows(loss_field, my_quantiles, BANDS)
    my_tables = upper_tail[:, None] + jnp.dot(window, upper_tri, precision=highest)
    tables = gather_directly(my_tables, "obl", 0).reshape(scen_count, sec_local, BANDS)
    all_tables = gather_directly(tables, "sector", 1)
    live_count = live_rows[0, 0]
    cap_rows = bands.shape[0]
    live_mask = jnp.arange(cap_rows, dtype=jnp.int32) < live_count
    exposure = bands.astype(jnp.float32)
    scaled = jnp.where(
        live_mask[None, :],
        weights.astype(jnp.float32) * (default_prob * exposure / 256.0)[None, :],
        0.0,
    )
    obligor_contrib, partial_value = tail_lookup(
        all_tables, scaled, jnp.where(live_mask, bands - 1, 0)
    )
    sector_part = summed_on_arrival(partial_value, "sector", 1)
    sector_total = taken_together(sector_part, "obl")
    obligors = OBL_DEV * lax.axis_size("sector") * obl_count
    sector_share = sector_total * (all_tables.shape[1] / obligors)
    return (obligor_contrib, sector_share)


def solution(mesh):
    in_specs = (
        P(None, None, "sector", "obl"),
        P(),
        P(("sector", "obl")),
        P(("sector", "obl")),
        P(None, ("sector", "obl")),
        P("sector", "obl"),
    )
    out_specs = (P(None, ("sector", "obl")), P(None, "sector"))
    return jax.shard_map(
        on_device, mesh=mesh, in_specs=in_specs, out_specs=out_specs, check_vma=False
    )
```

profile of v0, /device:TPU:1, one launch (start us, length us, event | category | flops | bytes accessed | tf_op | source)
XLA Modules:
  0.0 124.9 jit_solution(13181086647641620520)
XLA Ops:
  0.7 2.3 %copy.11 = f32[2,8,2,4096]{3,0,2,1:T(2,128)} copy(f32[2,8,2,4096]{3,2,1,0:T(2,128)} %param.8) | data formatting | bytes 1048576 | tf_op args[0]
  3.0 10.0 %all-to-all-start = ((f32[2,16,4096]{2,0,1:T(2,128)}), f32[2,16,4096]{2,0,1:T(2,128)S(1)}, u32[]{:S(2)}, u32[]{:S(2)}) async-start(f32[2,16,4096]{2,0,1:T(2,128)} %bitcast.2), calls=%async_computation | async-start | bytes 1048576 | tf_op jit(solution)/shard_map/all_to_all | solution.py:138
  15.1 15.1 %all-to-all-done = f32[2,16,4096]{2,0,1:T(2,128)S(1)} async-done(((f32[2,16,4096]{2,0,1:T(2,128)}), f32[2,16,4096]{2,0,1:T(2,128)S(1)}, u32[]{:S(2)}, u32[]{:S(2)}) %all-to-all-start) | async-done | bytes 524320 | tf_op jit(solution)/shard_map/all_to_all | solution.py:138
  30.2 1.4 %slice_reduce_fusion = (f32[16,4096]{1,0:T(8,128)S(1)}, f32[16,4096]{1,0:T(8,128)S(1)}) fusion(f32[2,16,4096]{2,0,1:T(2,128)S(1)} %all-to-all-done), kind=kLoop, calls=%fused_computation.25 | loop fusion | bytes 1048576 | tf_op jit(solution)/shard_map/slice | solution.py:141
  31.6 1.8 %fusion.33 = f32[256,256]{1,0:T(8,128)S(1)} fusion(f32[256,256]{1,0:T(8,128)S(1)} %reshape.159), kind=kOutput, calls=%fused_computation.47 | convolution fusion | flops 202244096 | bytes 524288 | tf_op jit(solution)/shard_map/kab,ac->ckb/dot_general | solution.py:57
  33.3 1.8 %fusion.36 = f32[256,256]{1,0:T(8,128)S(1)} fusion(f32[256,256]{1,0:T(8,128)S(1)} %reshape.159), kind=kOutput, calls=%fused_computation.48 | convolution fusion | flops 202244096 | bytes 524288 | tf_op jit(solution)/shard_map/kab,ac->ckb/dot_general | solution.py:60
  35.2 1.8 %convolution_subtract_fusion.1 = f32[256,256]{1,0:T(8,128)S(1)} fusion(f32[256,256]{1,0:T(8,128)S(1)} %fusion.33, f32[256,256]{1,0:T(8,128)S(1)} %reshape.160), kind=kOutput, calls=%fused_computation.17 | convolution fusion | flops 202309632 | bytes 786432 | tf_op jit(solution)/shard_map/kab,ac->ckb/dot_general | solution.py:57
  36.9 1.8 %convolution_add_fusion = f32[256,256]{1,0:T(8,128)S(1)} fusion(f32[256,256]{1,0:T(8,128)S(1)} %fusion.36, f32[256,256]{1,0:T(8,128)S(1)} %reshape.160), kind=kOutput, calls=%fused_computation.16 | convolution fusion | flops 202309632 | bytes 786432 | tf_op jit(solution)/shard_map/kab,ac->ckb/dot_general | solution.py:60
  38.7 2.4 %fusion.14 = f32[256,256]{1,0:T(8,128)S(1)} fusion(f32[256,256]{1,0:T(8,128)S(1)} %convolution_add_fusion, f32[256,256]{1,0:T(8,128)S(1)} %convolution_subtract_fusion.1), kind=kOutput, calls=%fused_computation.31 | convolution fusion | flops 202637312 | bytes 786432 | tf_op jit(solution)/shard_map/ckb,bd->kdc/dot_general | solution.py:78
  41.1 3.7 %select_reduce_fusion = (f32[]{:T(128)}, f32[256,256]{1,0:T(8,128)S(1)}) fusion(s32[]{:T(128)} %bitcast.1, f32[256,256]{1,0:T(8,128)S(1)} %fusion.14, f32[256,256]{1,0:T(8,128)S(1)} %convolution_add_fusion, f32[256,256]{1,0:T(8,128)S(1)} %convolution_subtract_fusion.1), kind=kOutput, calls=%fused_computation.27 | convolution fusion | flops 203096064 | bytes 1048584 | tf_op jit(solution)/shard_map/ckb,bd->kdc/dot_general | solution.py:78
  44.9 6.2 %gather_fusion = f32[1024]{0:T(1024)S(1)} fusion(f32[65536]{0:T(1024)S(1)} %bitcast.38, s32[1024]{0:T(1024)S(1)} %broadcast_clamp_fusion), kind=kCustom, calls=%fused_computation | custom fusion | bytes 12288 | tf_op jit(solution)/shard_map/jit(take_along_axis)/gather | solution.py:93
  53.0 3.6 %all-to-all-start.1 = ((f32[16,1,1024]{2,1,0:T(1,128)}), f32[16,1,1024]{2,1,0:T(1,128)S(1)}, u32[]{:S(2)}, u32[]{:S(2)}) async-start(f32[16,1,1024]{2,1,0:T(1,128)} %broadcast_in_dim.88), calls=%async_computation.1 | async-start | bytes 131072 | tf_op jit(solution)/shard_map/all_to_all | solution.py:15
  56.6 7.1 %all-to-all-done.1 = f32[16,1,1024]{2,1,0:T(1,128)S(1)} async-done(((f32[16,1,1024]{2,1,0:T(1,128)}), f32[16,1,1024]{2,1,0:T(1,128)S(1)}, u32[]{:S(2)}, u32[]{:S(2)}) %all-to-all-start.1) | async-done | bytes 65568 | tf_op jit(solution)/shard_map/all_to_all | solution.py:15
  63.9 1.4 %broadcast_in_dim.90 = f32[16,8,2,1024]{3,2,1,0:T(2,128)} broadcast(f32[8,2,1024]{2,1,0:T(2,128)S(1)} %broadcast_in_dim.89), dimensions={1,2,3} | broadcast | bytes 1114112 | tf_op jit(solution)/shard_map/broadcast_in_dim | solution.py:16
  65.3 6.9 %all-to-all-start.2 = ((f32[16,8,2,1024]{3,2,1,0:T(2,128)}), f32[16,8,2,1024]{3,2,1,0:T(2,128)S(1)}, u32[]{:S(2)}, u32[]{:S(2)}) async-start(f32[16,8,2,1024]{3,2,1,0:T(2,128)} %broadcast_in_dim.90), calls=%async_computation.2 | async-start | bytes 2097152 | tf_op jit(solution)/shard_map/all_to_all | solution.py:15
  72.3 16.4 %all-to-all-done.2 = f32[16,8,2,1024]{3,2,1,0:T(2,128)S(1)} async-done(((f32[16,8,2,1024]{3,2,1,0:T(2,128)}), f32[16,8,2,1024]{3,2,1,0:T(2,128)S(1)}, u32[]{:S(2)}, u32[]{:S(2)}) %all-to-all-start.2) | async-done | bytes 1048608 | tf_op jit(solution)/shard_map/all_to_all | solution.py:15
  89.6 12.3 %while.16 = (s32[]{:T(128)}, f32[8,4096]{1,0:T(8,128)S(1)}, f32[8,32]{1,0:T(8,128)S(1)}, f32[32,4096]{1,0:T(8,128)S(1)}, s32[4096]{0:T(1024)S(1)}, /*index=5*/f3...) while((s32[]{:T(128)}, f32[8,4096]{1,0:T(8,128)S(1)}, ...), condition=%wide.region_4.5_spmd.clone, body=%wide.region_1.4_spmd.clone.sunk | while | flops 1611657472 | bytes 2420905 | solution.py:122
  89.7 1.2 multiply_reduce_fusion.2
  91.2 1.2 multiply_reduce_fusion.2
  92.7 1.2 multiply_reduce_fusion.2
  94.3 1.2 multiply_reduce_fusion.2
  97.3 1.2 multiply_reduce_fusion.2
  101.9 10.7 %all_to_all.29 = f32[16,8,2]{1,2,0:T(2,128)S(1)} all-to-all(f32[16,8,2]{1,2,0:T(2,128)S(1)} %bitcast.41), channel_id=1, replica_groups=mesh['sector'=16,'obl'=16] {'sector'}, dimensions={0} | all-to-all | bytes 2048 | tf_op jit(solution)/shard_map/all_to_all | solution.py:39
  112.6 11.7 %all_to_all.30 = f32[16,8,2]{1,2,0:T(2,128)S(1)} all-to-all(f32[16,8,2]{1,2,0:T(2,128)S(1)} %broadcast_in_dim.91), channel_id=1, replica_groups=mesh['sector'=16,'obl'=16] {'obl'}, dimensions={0} | all-to-all | bytes 2048 | tf_op jit(solution)/shard_map/all_to_all | solution.py:15
  (88 shorter events, 10.8 us)
Async XLA Ops:
  0.6 12.3 %copy-start.4 = (s32[8]{0:T(128)S(1)}, s32[8]{0:T(128)}, u32[]{:S(2)}) copy-start(s32[8]{0:T(128)} %param.9) | copy-start | bytes 100
  0.6 14.4 %copy-start.2 = (s32[4096]{0:T(1024)S(1)}, s32[4096]{0:T(1024)}, u32[]{:S(2)}) copy-start(s32[4096]{0:T(1024)} %param.10) | copy-start | bytes 49156
  0.7 14.4 %copy-start.3 = (f32[4096]{0:T(1024)S(1)}, f32[4096]{0:T(1024)}, u32[]{:S(2)}) copy-start(f32[4096]{0:T(1024)} %param.11) | copy-start | bytes 49156
  3.0 27.2 %all-to-all-start = ((f32[2,16,4096]{2,0,1:T(2,128)}), f32[2,16,4096]{2,0,1:T(2,128)S(1)}, u32[]{:S(2)}, u32[]{:S(2)}) async-start(f32[2,16,4096]{2,0,1:T(2,128)} %bitcast.2), calls=%async_computation | async-start | bytes 1048576 | tf_op jit(solution)/shard_map/all_to_all | solution.py:138
  53.0 10.7 %all-to-all-start.1 = ((f32[16,1,1024]{2,1,0:T(1,128)}), f32[16,1,1024]{2,1,0:T(1,128)S(1)}, u32[]{:S(2)}, u32[]{:S(2)}) async-start(f32[16,1,1024]{2,1,0:T(1,128)} %broadcast_in_dim.88), calls=%async_computation.1 | async-start | bytes 131072 | tf_op jit(solution)/shard_map/all_to_all | solution.py:15
  65.3 6.9 %copy-start = (s32[32,4096]{1,0:T(8,128)S(1)}, s32[32,4096]{1,0:T(8,128)}, u32[]{:S(2)}) copy-start(s32[32,4096]{1,0:T(8,128)} %param.12) | copy-start | bytes 1572868
  65.3 23.4 %all-to-all-start.2 = ((f32[16,8,2,1024]{3,2,1,0:T(2,128)}), f32[16,8,2,1024]{3,2,1,0:T(2,128)S(1)}, u32[]{:S(2)}, u32[]{:S(2)}) async-start(f32[16,8,2,1024]{3,2,1,0:T(2,128)} %broadcast_in_dim.90), calls=%async_computation.2 | async-start | bytes 2097152 | tf_op jit(solution)/shard_map/all_to_all | solution.py:15
  101.8 23.1 %copy-start.1 = (f32[8,4096]{1,0:T(8,128)}, f32[8,4096]{1,0:T(8,128)S(1)}, u32[]{:S(2)}) copy-start(f32[8,4096]{1,0:T(8,128)S(1)} %get-tuple-element.125) | copy-start | bytes 393220
where the time goes:
time: 125 us
  waiting for transfers between devices  38.5 us (31%)
  matrix products  23.5 us (19%)
  blocking collectives  22.4 us (18%)
  starting transfers between devices  20.4 us (16%)
  local copies, waits for them, and re-layouts  15.2 us (12%)
  other arithmetic  2.46 us (2%)
  between operations  2.18 us (2%)
    all_to_all x2, waiting for transfers between devices, sent_to_all(): lax.all_to_all(jnp.broadcast_to(value[None], (peers, *value.shape)), axis...  23.5 us
    all_to_all x1, waiting for transfers between devices, on_device(): lax.all_to_all(flat_spectra, 'obl', split_axis=1, concat_axis=2, tiled=True)  15.1 us
    all_to_all x1, blocking collectives, sent_to_all(): lax.all_to_all(jnp.broadcast_to(value[None], (peers, *value.shape)), axis...  11.7 us
    all_to_all x1, blocking collectives, summed_on_arrival(): lax.all_to_all(cut_along(value, dim, peers), axis, 0, 0, tiled=True)  10.7 us
    all_to_all x2, starting transfers between devices, sent_to_all(): lax.all_to_all(jnp.broadcast_to(value[None], (peers, *value.shape)), axis...  10.5 us
    all_to_all x1, starting transfers between devices, on_device(): lax.all_to_all(flat_spectra, 'obl', split_axis=1, concat_axis=2, tiled=True)  9.97 us
    dot_general x8, matrix products, block_step(): jnp.dot(flat_tables, one_hot, precision=highest)  9.66 us
    gather x1, local copies, waits for them, and re-layouts, whole_rows(): window = jnp.take_along_axis(loss_field, index_table, axis=1)  6.15 us
  transfers between devices with their start and end apart: 3, of which 3 were waited for; matrix products, arithmetic and copies ran while one was open for 1% of the time, Pallas kernels for 0%

commit v1 on v0

v1 whole, which is shorter than its diff:
```python
import math

import jax
import jax.numpy as jnp
from jax import lax
from jax.experimental import pallas as pl
from jax.experimental.pallas import tpu as pltpu
from jax.sharding import PartitionSpec as P

GRID = 65536
BANDS = 1024
OBL_DEV = 1024
LANES = 128
HALF = BANDS // 2
A_LEN = 32
BLOCK = 512
F32 = jnp.float32
BF16 = jnp.bfloat16
I32 = jnp.int32


def iota(shape, dim):
    return lax.broadcasted_iota(I32, shape, dim)


def cos_sin(turns, log_grid):
    quarter_log = log_grid - 2
    quadrant = (turns + (1 << (quarter_log - 1))) >> quarter_log
    rest = turns - (quadrant << quarter_log)
    x = rest.astype(F32) * F32(2.0 * math.pi / (1 << log_grid))
    y = x * x
    sine = x * (1.0 + y * (-1.0 / 6 + y * (1.0 / 120 + y * (-1.0 / 5040 + y * (1.0 / 362880)))))
    cosine = 1.0 + y * (
        -0.5 + y * (1.0 / 24 + y * (-1.0 / 720 + y * (1.0 / 40320 - y * (1.0 / 3628800))))
    )
    odd = (quadrant & 1) == 1
    first = jnp.where(odd, cosine, sine)
    second = jnp.where(odd, sine, cosine)
    return (
        jnp.where(((quadrant + 1) & 2) == 2, -second, second),
        jnp.where((quadrant & 2) == 2, -first, first),
    )


def two_parts(value):
    high = value.astype(BF16).astype(F32)
    return high, value - high


def spectral_kernel(place, quantile, spec, mine, other, lhs, grid, turn_cos, turn_sin, table, offset):
    part = place[0]
    core = place[1]
    scen = spec.shape[1]
    rows = 2 * scen
    shape = (A_LEN, LANES)
    freq = part * (A_LEN * LANES) + iota(shape, 0) * LANES + iota(shape, 1)
    zero = freq == 0
    half_cos, half_sin = cos_sin(freq, 17)
    v_im = jnp.where(zero, 0.0, 0.5 * half_cos / jnp.where(zero, 1.0, half_sin))
    v_re = jnp.where(zero, 0.0, 0.5)
    band_lane = iota((1, LANES), 1)
    for c in range(scen):
        q_less = quantile[c] - 1
        w_cos, w_sin = cos_sin((freq * q_less) & (GRID - 1), 16)
        u_re = v_re * w_cos - v_im * w_sin
        u_im = v_re * w_sin + v_im * w_cos
        for k in range(2):
            x_re = spec[0, c, pl.ds(k, A_LEN, stride=2), :]
            x_im = spec[1, c, pl.ds(k, A_LEN, stride=2), :]
            z_re = x_re * u_re - x_im * u_im
            z_im = x_re * u_im + x_im * u_re
            re_high, re_low = two_parts(z_re)
            im_high, im_low = two_parts(z_im)
            turned = jnp.concatenate([re_high, im_high, re_low, im_low], 0).T.astype(BF16)
            row = k * scen + c
            lhs[row * LANES : (row + 1) * LANES, :LANES] = turned
            lhs[row * LANES : (row + 1) * LANES, LANES:] = turned
            total = jnp.sum(x_re * v_re - x_im * v_im)
            at_zero = jnp.where(part == 0, x_re[0:1, 0:1], 0.0)
            line = at_zero * (GRID - q_less + band_lane).astype(F32) - total
            offset[row : row + 1, :] = line
            offset[rows + row : rows + row + 1, :] = jnp.broadcast_to(at_zero, (1, LANES))
    d_shape = (A_LEN, HALF)
    d_turn = ((part * A_LEN + iota(d_shape, 0)) * iota(d_shape, 1)) & (HALF - 1)
    d_cos, d_sin = cos_sin(d_turn, 9)
    dft = jnp.concatenate(
        [jnp.concatenate([d_cos, -d_sin], 1), jnp.concatenate([d_sin, d_cos], 1)], 0
    )
    d_high, d_low = two_parts(dft)
    d_high = d_high.astype(BF16)
    d_low = d_low.astype(BF16)
    table[...] = jnp.concatenate([d_high, d_high, d_low, d_low], 0)
    t_shape = (LANES, LANES)
    run_cos, run_sin = cos_sin(iota(t_shape, 0) * iota(t_shape, 1), 16)
    step_cos, step_sin = cos_sin(iota(t_shape, 0) * LANES, 16)
    for m in range(8):
        turn_cos[:, m * LANES : (m + 1) * LANES] = run_cos
        turn_sin[:, m * LANES : (m + 1) * LANES] = run_sin
        run_cos, run_sin = (
            run_cos * step_cos - run_sin * step_sin,
            run_sin * step_cos + run_cos * step_sin,
        )
    group = 4
    for g in range(rows // group):
        grid[...] = jnp.dot(
            lhs[g * group * LANES : (g + 1) * group * LANES, :],
            table[...],
            preferred_element_type=F32,
        )

        def tile(t, _):
            lane = pl.multiple_of(t * LANES, LANES)
            for h in range(2):
                acc = [None] * group
                for b in range(LANES // 8):
                    tc = turn_cos[b * 8 : (b + 1) * 8, pl.ds(h * HALF + lane, LANES)]
                    ts = turn_sin[b * 8 : (b + 1) * 8, pl.ds(h * HALF + lane, LANES)]
                    for r in range(group):
                        at = r * LANES + b * 8
                        term = (
                            grid[at : at + 8, pl.ds(lane, LANES)] * tc
                            + grid[at : at + 8, pl.ds(HALF + lane, LANES)] * ts
                        )
                        acc[r] = term if acc[r] is None else acc[r] + term
                for r in range(group):
                    row = g * group + r
                    line = jnp.sum(acc[r], axis=0, keepdims=True)
                    moved = (h * HALF + lane).astype(F32)
                    line = line + offset[row : row + 1, :]
                    line = line + offset[rows + row : rows + row + 1, :] * moved
                    line = line * F32(1.0 / GRID)

                    @pl.when(core == h)
                    def _():
                        mine[pl.ds(t * rows + row, 1), :] = line

                    @pl.when(core != h)
                    def _():
                        other[pl.ds(t * rows + row, 1), :] = line

            return 0

        lax.fori_loop(0, HALF // LANES, tile, 0)


def spectral(place, quantile, spec):
    scen = spec.shape[1]
    rows = 2 * scen
    smem = pl.BlockSpec(memory_space=pltpu.SMEM)
    vmem = pl.BlockSpec(memory_space=pltpu.VMEM)
    out = jax.ShapeDtypeStruct((HALF // LANES * rows, LANES), F32)
    return pl.pallas_call(
        spectral_kernel,
        out_shape=(out, out),
        in_specs=[smem, smem, vmem],
        out_specs=(vmem, vmem),
        scratch_shapes=[
            pltpu.VMEM((rows * LANES, 2 * LANES), BF16),
            pltpu.VMEM((4 * LANES, 2 * HALF), F32),
            pltpu.VMEM((LANES, BANDS), F32),
            pltpu.VMEM((LANES, BANDS), F32),
            pltpu.VMEM((2 * LANES, 2 * HALF), BF16),
            pltpu.VMEM((2 * rows, LANES), F32),
        ],
        cost_estimate=pl.CostEstimate(flops=3_000_000_000, bytes_accessed=600_000, transcendentals=0),
        name="spectral",
    )(place, quantile, spec)


def slot_factor(bands, prob):
    return prob * bands.astype(F32) / 256.0


def band_weights_kernel(live, bands, prob, weights, out, acc):
    sectors = weights.shape[0]
    acc[...] = jnp.zeros_like(acc)

    def block(n, _):
        at = pl.multiple_of(n * BLOCK, BLOCK)
        band = bands[:, pl.ds(at, BLOCK)]
        factor = slot_factor(band, prob[:, pl.ds(at, BLOCK)])
        alive = at + iota((1, BLOCK), 1) < live[0]
        factor = jnp.where(alive, factor, 0.0)
        index = band - 1
        low = index & 255
        high = index >> 8
        value = weights[:, pl.ds(at, BLOCK)].astype(F32) * factor
        v_high, v_low = two_parts(value)
        pieces = []
        for h in range(4):
            here = high == h
            pieces.append(jnp.where(here, v_high, 0.0).astype(BF16))
            pieces.append(jnp.where(here, v_low, 0.0).astype(BF16))
        left = jnp.concatenate(pieces, 0)
        hot = (iota((256, BLOCK), 0) == low).astype(F32).astype(BF16)
        acc[...] += lax.dot_general(
            left, hot, (((1,), (1,)), ((), ())), preferred_element_type=F32
        )
        return 0

    lax.fori_loop(0, (live[0] + BLOCK - 1) // BLOCK, block, 0)
    for h in range(4):
        both = acc[h * 2 * sectors : (h * 2 + 1) * sectors, :] + acc[
            (h * 2 + 1) * sectors : (h * 2 + 2) * sectors, :
        ]
        out[:, 2 * h, :] = both[:, :LANES]
        out[:, 2 * h + 1, :] = both[:, LANES:]


def band_weights(live, bands, prob, weights):
    sectors = weights.shape[0]
    smem = pl.BlockSpec(memory_space=pltpu.SMEM)
    vmem = pl.BlockSpec(memory_space=pltpu.VMEM)
    return pl.pallas_call(
        band_weights_kernel,
        out_shape=jax.ShapeDtypeStruct((sectors, BANDS // LANES, LANES), F32),
        in_specs=[smem, vmem, vmem, vmem],
        out_specs=vmem,
        scratch_shapes=[pltpu.VMEM((8 * sectors, 256), F32)],
        cost_estimate=pl.CostEstimate(flops=600_000_000, bytes_accessed=700_000, transcendentals=0),
        name="band_weights",
    )(live, bands, prob, weights)


def spread_kernel(mine, got, out):
    value = mine[...] + got[...]
    for n in range(out.shape[0]):
        out[n] = value


def spread(mine, got, copies):
    return pl.pallas_call(
        spread_kernel,
        out_shape=jax.ShapeDtypeStruct((copies, *mine.shape), F32),
        name="spread",
    )(mine, got)


def join_kernel(parts, sums, out):
    value = parts[0]
    for n in range(1, parts.shape[0]):
        value = value + parts[n]
    rows = value.shape[0]
    for n in range(out.shape[0]):
        out[n, :rows, :] = value
        out[n, rows:, :] = sums[n]


def join(parts, sums):
    peers, extra, lanes = sums.shape
    return pl.pallas_call(
        join_kernel,
        out_shape=jax.ShapeDtypeStruct((peers, parts.shape[1] + extra, lanes), F32),
        name="join",
    )(parts, sums)


def lookup_kernel(*refs, last):
    if last:
        place, live, tables, bands, prob, weights, before, out, lhs = refs
    else:
        place, live, tables, bands, weights, out, lhs = refs
    peers = tables.shape[0]
    rows = HALF // LANES
    each = 16
    count = peers * each
    sectors = weights.shape[0]
    for t in range(rows):
        value = tables[:, t * each : (t + 1) * each, :].reshape(count, LANES)
        high, low = two_parts(value)
        lhs[:count, t * LANES : (t + 1) * LANES] = high.astype(BF16)
        lhs[count:, t * LANES : (t + 1) * LANES] = low.astype(BF16)
    first = place[1] * HALF if not last else (1 - place[1]) * HALF
    blocks = (live[0] + BLOCK - 1) // BLOCK

    def block(n, _):
        at = pl.multiple_of(n * BLOCK, BLOCK)
        band = bands[:, pl.ds(at, BLOCK)]
        hot = (iota((HALF, BLOCK), 0) == band - 1 - first).astype(F32).astype(BF16)
        found = jnp.dot(lhs[...], hot, preferred_element_type=F32)
        weight = weights[:, pl.ds(at, BLOCK)].astype(F32)
        scen = count // sectors
        acc = jnp.zeros((scen, BLOCK), F32)
        for k in range(sectors):
            entry = found[k * scen : (k + 1) * scen] + found[count + k * scen : count + (k + 1) * scen]
            acc = acc + entry * weight[k : k + 1, :]
        if last:
            factor = slot_factor(band, prob[:, pl.ds(at, BLOCK)])
            alive = at + iota((1, BLOCK), 1) < live[0]
            acc = jnp.where(alive, (acc + before[:, pl.ds(at, BLOCK)]) * factor, 0.0)
        out[:, pl.ds(at, BLOCK)] = acc
        return 0

    lax.fori_loop(0, blocks, block, 0)
    if last:

        def empty(n, _):
            at = pl.multiple_of(n * BLOCK, BLOCK)
            out[:, pl.ds(at, BLOCK)] = jnp.zeros((out.shape[0], BLOCK), F32)
            return 0

        lax.fori_loop(blocks, out.shape[1] // BLOCK, empty, 0)


def lookup(place, live, tables, bands, prob, weights, before):
    import functools

    last = before is not None
    slots = bands.shape[1]
    sectors = weights.shape[0]
    scen = tables.shape[0] * 16 // sectors
    smem = pl.BlockSpec(memory_space=pltpu.SMEM)
    vmem = pl.BlockSpec(memory_space=pltpu.VMEM)
    args = [place, live, tables, bands] + ([prob] if last else []) + [weights] + ([before] if last else [])
    return pl.pallas_call(
        functools.partial(lookup_kernel, last=last),
        out_shape=jax.ShapeDtypeStruct((scen, slots), F32),
        in_specs=[smem, smem] + [vmem] * (len(args) - 2),
        out_specs=vmem,
        scratch_shapes=[pltpu.VMEM((tables.shape[0] * 32, HALF), BF16)],
        cost_estimate=pl.CostEstimate(flops=4_300_000_000, bytes_accessed=1_000_000, transcendentals=0),
        name="lookup_last" if last else "lookup_first",
    )(*args)


def share_kernel(place, near, far, out):
    core = place[1]
    peers = near.shape[0]
    sums = near[0, 64:, :]
    for n in range(1, peers):
        sums = sums + near[n, 64:, :]
    near_rows = near[place[2], :64, :]
    far_rows = far[place[2], :64, :]
    acc = [jnp.zeros((8, LANES), F32) for _ in range(2)]
    for t in range(4):
        for h in range(2):
            block = jnp.where(core == h, near_rows[t * 16 : (t + 1) * 16], far_rows[t * 16 : (t + 1) * 16])
            for k in range(2):
                chunk = h * 4 + t
                acc[k] = acc[k] + block[k * 8 : (k + 1) * 8] * sums[k * 8 + chunk : k * 8 + chunk + 1, :]
    both = jnp.concatenate(acc + [jnp.zeros((LANES - 16, LANES), F32)], 0).T
    line = jnp.sum(both, axis=0, keepdims=True)
    for n in range(out.shape[0]):
        out[n] = line


def share(place, near, far, copies):
    smem = pl.BlockSpec(memory_space=pltpu.SMEM)
    vmem = pl.BlockSpec(memory_space=pltpu.VMEM)
    return pl.pallas_call(
        share_kernel,
        out_shape=jax.ShapeDtypeStruct((copies, 1, LANES), F32),
        in_specs=[smem, vmem, vmem],
        out_specs=vmem,
        name="share",
    )(place, near, far)


def on_device(spectrum, quantile_index, bands, default_prob, weights, live_rows):
    scen, sec_local = spectrum.shape[1], spectrum.shape[2]
    n_obl = lax.axis_size("obl")
    n_sector = lax.axis_size("sector")
    part = lax.axis_index("obl").astype(I32)
    place = jnp.stack([part, part & 1, lax.axis_index("sector").astype(I32)])
    live = live_rows.reshape(1)
    spec = spectrum.reshape(2, scen, sec_local, A_LEN, LANES).transpose(0, 1, 3, 2, 4)
    spec = spec.reshape(2, scen, A_LEN * sec_local, LANES)
    bands = bands[None, :]
    prob = default_prob[None, :]
    swap = [(n, n ^ 1) for n in range(n_obl)]
    same_core = [[n for n in range(n_obl) if n % 2 == c] for c in range(2)]

    mine, other = spectral(place, quantile_index, spec)
    got = lax.ppermute(other, "obl", swap)
    copies = spread(mine, got, n_obl // 2)
    parts = lax.all_to_all(copies, "obl", 0, 0, axis_index_groups=same_core, tiled=True)
    sums = band_weights(live, bands, prob, weights).reshape(n_sector, 16, LANES)
    near = lax.all_to_all(join(parts, sums), "sector", 0, 0, tiled=True)
    far = lax.ppermute(near, "obl", swap)
    before = lookup(place, live, near, bands, prob, weights, None)
    shares = lax.all_to_all(share(place, near, far, n_obl), "obl", 0, 0, tiled=True)
    contrib = lookup(place, live, far, bands, prob, weights, before)
    obligors = OBL_DEV * n_sector * n_obl
    total = jnp.sum(shares, axis=0)[0, : sec_local * scen].reshape(sec_local, scen).T
    return contrib, total * (sec_local * n_sector / obligors)


def solution(mesh):
    in_specs = (
        P(None, None, "sector", "obl"),
        P(),
        P(("sector", "obl")),
        P(("sector", "obl")),
        P(None, ("sector", "obl")),
        P("sector", "obl"),
    )
    out_specs = (P(None, ("sector", "obl")), P(None, "sector"))
    return jax.shard_map(
        on_device, mesh=mesh, in_specs=in_specs, out_specs=out_specs, check_vma=False
    )
```

time: 125 us -> 75.4 us (0.60)
  waiting for transfers between devices: 38.5 us -> 13.3 us
  matrix products: 23.5 us -> 0 us
  Pallas kernels: 0 us -> 22 us
  local copies, waits for them, and re-layouts: 15.2 us -> 2.8 us
  blocking collectives: 22.4 us -> 18 us
  starting transfers between devices: 20.4 us -> 17.3 us
  other arithmetic: 2.46 us -> 0.64 us
    all_to_all x3 -> x2, waiting for transfers between devices: 38.5 us -> 12.2 us  [the longest x1 8.13 us: on_device(): lax.all_to_all(copies, 'obl', 0, 0, axis_index_groups=same_core, tiled=True)]
    dot_general x15 -> x0, matrix products: 23.5 us -> none  [the longest x8 9.66 us: block_step(): jnp.dot(flat_tables, one_hot, precision=highest)]
    pallas_call x0 -> x7, Pallas kernels: none -> 22 us  [the longest x1 8.3 us: spectral(): pl.pallas_call(spectral_kernel, out_shape=(out, out), in_specs=[smem, sme...]
    all_to_all x3 -> x2, starting transfers between devices: 20.4 us -> 11.4 us  [the longest x1 6.48 us: on_device(): lax.all_to_all(copies, 'obl', 0, 0, axis_index_groups=same_core, tiled=True)]
    gather x1 -> x0, local copies, waits for them, and re-layouts: 6.15 us -> none  [whole_rows(): window = jnp.take_along_axis(loss_field, index_table, axis=1)]
    ppermute x0 -> x2, starting transfers between devices: none -> 5.9 us  [the longest x1 3.19 us: on_device(): got = lax.ppermute(other, 'obl', swap)]
    all_to_all x2 -> x1, blocking collectives: 22.4 us -> 18 us  [on_device(): near = lax.all_to_all(join(parts, sums), 'sector', 0, 0, tiled=True)]
    broadcast_in_dim x6 -> x0, local copies, waits for them, and re-layouts: 2.19 us -> none  [the longest x4 2.11 us: sent_to_all(): jnp.broadcast_to(value[None], (peers, *value.shape))]
  transfers between devices with their start and end apart: 3 -> 4, of which waited for: 3 -> 3; matrix products, arithmetic and copies ran while one was open for 1% -> 0% of each run, Pallas kernels for 0% -> 11%
where the time goes in v1:
time: 75.4 us; the launch traced here: 75.3 us
  Pallas kernels  22 us (29%)
  blocking collectives  18 us (24%)
  starting transfers between devices  17.3 us (23%)
  waiting for transfers between devices  13.3 us (18%)
  local copies, waits for them, and re-layouts  2.8 us (4%)
  between operations  1.3 us (2%)
    all_to_all x1, blocking collectives, on_device(): near = lax.all_to_all(join(parts, sums), 'sector', 0, 0, tiled=True)  18 us
    pallas_call x1, Pallas kernels, spectral(): pl.pallas_call(spectral_kernel, out_shape=(out, out), in_specs=[smem, sme...  8.3 us
    all_to_all x1, waiting for transfers between devices, on_device(): lax.all_to_all(copies, 'obl', 0, 0, axis_index_groups=same_core, tiled=True)  8.13 us
    all_to_all x1, starting transfers between devices, on_device(): lax.all_to_all(copies, 'obl', 0, 0, axis_index_groups=same_core, tiled=True)  6.48 us
    pallas_call x2, Pallas kernels, lookup(): pl.pallas_call(functools.partial(lookup_kernel, last=last), out_shape=jax...  5.86 us
    all_to_all x1, starting transfers between devices, on_device(): lax.all_to_all(share(place, near, far, n_obl), 'obl', 0, 0, tiled=True)  4.9 us
    all_to_all x1, waiting for transfers between devices, on_device(): lax.all_to_all(share(place, near, far, n_obl), 'obl', 0, 0, tiled=True)  4.08 us
    ppermute x1, starting transfers between devices, on_device(): got = lax.ppermute(other, 'obl', swap)  3.19 us
  transfers between devices with their start and end apart: 4, of which 3 were waited for; matrix products, arithmetic and copies ran while one was open for 0% of the time, Pallas kernels for 11%

profile of v1, /device:TPU:1, one launch (start us, length us, event | category | flops | bytes accessed | tf_op | source)
XLA Modules:
  0.0 75.3 jit_solution(10195857225538501735)
XLA Ops:
  0.6 0.6 pad_add_fusion.place.refs_0_
  1.2 8.3 %spectral.1 = (f32[64,128]{1,0:T(8,128)}, f32[64,128]{1,0:T(8,128)}) custom-call(s32[3]{0:T(128)} %pad_add_fusion.place.refs_0_, s32[8]{0:T(128)} %quantile.1, f32[2,8,64,128]{3,2,1,0:T(8,128)} %bitcast.19), custom_call_target="tpu_custom_call" | custom-call | flops 3000000000 | bytes 600000 | tf_op jit(solution)/shard_map/spectral/pallas_call | solution.py:152
  9.5 3.2 %collective-permute-start = (f32[64,128]{1,0:T(8,128)}, f32[64,128]{1,0:T(8,128)S(1)}, u32[]{:S(2)}, u32[]{:S(2)}) collective-permute-start(f32[64,128]{1,0:T(8,128)} %get-tuple-element.5), channel_id=1, source_target_pairs={{0,1},{1,0},{2,3},{3,2},{4,5},{5,4},{6,7},{7,6},{8,9},{9,8},{10,11... | collective-permute-start | bytes 98312 | tf_op jit(solution)/shard_map/ppermute | solution.py:374
  12.7 1.1 %collective-permute-done.got = f32[64,128]{1,0:T(8,128)S(1)} collective-permute-done((f32[64,128]{1,0:T(8,128)}, f32[64,128]{1,0:T(8,128)S(1)}, u32[]{:S(2)}, u32[]{:S(2)}) %collective-permute-start) | collective-permute-done | bytes 32800 | tf_op jit(solution)/shard_map/ppermute | solution.py:374
  13.8 0.0 copy-start.3
  13.8 0.6 copy-done.3
  14.4 1.5 %spread.1 = f32[8,64,128]{2,1,0:T(8,128)} custom-call(f32[64,128]{1,0:T(8,128)} %get-tuple-element.4.mine, f32[64,128]{1,0:T(8,128)} %copy-done.3), custom_call_target="tpu_custom_call" | custom-call | tf_op jit(solution)/shard_map/spread/pallas_call | solution.py:232
  15.9 6.5 %all-to-all-start = ((f32[8,64,128]{2,1,0:T(8,128)}), f32[8,64,128]{2,1,0:T(8,128)S(1)}, u32[]{:S(2)}, u32[]{:S(2)}) async-start(f32[8,64,128]{2,1,0:T(8,128)} %spread.1), calls=%async_computation | async-start | bytes 524288 | tf_op jit(solution)/shard_map/all_to_all | solution.py:376
  23.0 2.4 %band_weights.1 = f32[32,8,128]{2,1,0:T(8,128)} custom-call(s32[1]{0:T(128)} %bitcast.14.live, s32[1,4096]{1,0:T(1,128)} %bitcast.20, f32[1,4096]{1,0:T(1,128)} %bitcast.23, s32[32,4096]{1,0:T(8,128)} %refs_5_.1), custom_call_target="tpu_custom_call" | custom-call | flops 600000000 | bytes 700000 | tf_op jit(solution)/shard_map/band_weights/pallas_call | solution.py:214
  25.4 8.1 %all-to-all-done.parts = f32[8,64,128]{2,1,0:T(8,128)S(1)} async-done(((f32[8,64,128]{2,1,0:T(8,128)}), f32[8,64,128]{2,1,0:T(8,128)S(1)}, u32[]{:S(2)}, u32[]{:S(2)}) %all-to-all-start) | async-done | bytes 262176 | tf_op jit(solution)/shard_map/all_to_all | solution.py:376
  33.6 0.0 copy-start.1
  33.6 0.7 copy-done.1
  34.3 1.9 %join.1 = f32[16,80,128]{2,1,0:T(8,128)} custom-call(f32[8,64,128]{2,1,0:T(8,128)} %copy-done.1, f32[16,16,128]{2,1,0:T(8,128)} %bitcast.17), custom_call_target="tpu_custom_call" | custom-call | tf_op jit(solution)/shard_map/join/pallas_call | solution.py:251
  36.1 18.0 %all_to_all.15.refs_2_.near = f32[16,80,128]{2,1,0:T(8,128)S(1)} all-to-all(f32[16,80,128]{2,1,0:T(8,128)} %join.1), channel_id=1, replica_groups=mesh['sector'=16,'obl'=16] {'sector'}, dimensions={0} | all-to-all | bytes 1310720 | tf_op jit(solution)/shard_map/all_to_all | solution.py:378
  54.1 2.7 %collective-permute-start.1 = (f32[16,80,128]{2,1,0:T(8,128)S(1)}, f32[16,80,128]{2,1,0:T(8,128)S(1)}, u32[]{:S(2)}, u32[]{:S(2)}) collective-permute-start(f32[16,80,128]{2,1,0:T(8,128)S(1)} %all_to_all.15.refs_2_.near), channel_id=1, source_target_pairs={{0,1},{1,0},{2,3},{3,2},{4,5},{5,4},{6,7},{7,6},{8,9},{9,8},{10,11... | collective-permute-start | bytes 1966088 | tf_op jit(solution)/shard_map/ppermute | solution.py:379
  56.8 0.0 copy-done
  56.8 2.9 %lookup_first.1.refs_6_ = f32[8,4096]{1,0:T(8,128)} custom-call(s32[3]{0:T(128)} %pad_add_fusion.place.refs_0_, s32[1]{0:T(128)} %bitcast.15.refs_1_, f32[16,80,128]{2,1,0:T(8,128)} %copy-done, s32[1,4096]{1,0:T(1,128)} %bitcast.21, s32[32,4096]{1,0:T(8,128)} %refs_5_.1), custom_call_target="tpu_custom_call" | custom-call | flops 4300000256 | bytes 1000000 | tf_op jit(solution)/shard_map/lookup_first/pallas_call | solution.py:315
  59.7 0.0 collective-permute-done.1.refs_2_.far
  59.7 0.8 %copy-done.2 = f32[16,80,128]{2,1,0:T(8,128)} copy-done((f32[16,80,128]{2,1,0:T(8,128)}, f32[16,80,128]{2,1,0:T(8,128)S(1)}, u32[]{:S(2)}) %copy-start.2) | copy-done | bytes 655384
  60.6 2.0 %share.1 = f32[16,1,128]{2,1,0:T(1,128)} custom-call(s32[3]{0:T(128)} %pad_add_fusion.place.refs_0_, f32[16,80,128]{2,1,0:T(8,128)} %copy-done, f32[16,80,128]{2,1,0:T(8,128)} %copy-done.2), custom_call_target="tpu_custom_call" | custom-call | tf_op jit(solution)/shard_map/share/pallas_call | solution.py:350
  62.6 4.9 %all-to-all-start.2 = ((f32[16,1,128]{2,1,0:T(1,128)}), f32[16,1,128]{2,1,0:T(1,128)S(1)}, u32[]{:S(2)}, u32[]{:S(2)}) async-start(f32[16,1,128]{2,1,0:T(1,128)} %share.1), calls=%async_computation.2 | async-start | bytes 16384 | tf_op jit(solution)/shard_map/all_to_all | solution.py:381
  67.5 3.0 %lookup_last.1 = f32[8,4096]{1,0:T(8,128)} custom-call(s32[3]{0:T(128)} %pad_add_fusion.place.refs_0_, s32[1]{0:T(128)} %bitcast.16.refs_1_, f32[16,80,128]{2,1,0:T(8,128)} %copy-done.2, s32[1,4096]{1,0:T(1,128)} %bitcast.22, f32[1,4096]{1,0:T(1,128)} %bitcast.24, s32[32,4096]{1,0:T(8,128)} %refs_5_.1, f32[8,4096]{1,0:T(8,128)} %lookup_first.1.refs_6_), custom_call_target="tpu_custom_call" | custom-call | flops 4300000256 | bytes 1000000 | tf_op jit(solution)/shard_map/lookup_last/pallas_call | solution.py:315
  70.5 4.1 %all-to-all-done.2 = f32[16,1,128]{2,1,0:T(1,128)S(1)} async-done(((f32[16,1,128]{2,1,0:T(1,128)}), f32[16,1,128]{2,1,0:T(1,128)S(1)}, u32[]{:S(2)}, u32[]{:S(2)}) %all-to-all-start.2) | async-done | bytes 8224 | tf_op jit(solution)/shard_map/all_to_all | solution.py:381
  74.6 0.6 mul.10
  (4 shorter events, 0.1 us)
Async XLA Ops:
  9.5 4.3 %collective-permute-start = (f32[64,128]{1,0:T(8,128)}, f32[64,128]{1,0:T(8,128)S(1)}, u32[]{:S(2)}, u32[]{:S(2)}) collective-permute-start(f32[64,128]{1,0:T(8,128)} %get-tuple-element.5), channel_id=1, source_target_pairs={{0,1},{1,0},{2,3},{3,2},{4,5},{5,4},{6,7},{7,6},{8,9},{9,8},{10,11... | collective-permute-start | bytes 98312 | tf_op jit(solution)/shard_map/ppermute | solution.py:374
  13.8 0.6 copy-start.3
  15.9 17.7 %all-to-all-start = ((f32[8,64,128]{2,1,0:T(8,128)}), f32[8,64,128]{2,1,0:T(8,128)S(1)}, u32[]{:S(2)}, u32[]{:S(2)}) async-start(f32[8,64,128]{2,1,0:T(8,128)} %spread.1), calls=%async_computation | async-start | bytes 524288 | tf_op jit(solution)/shard_map/all_to_all | solution.py:376
  33.6 0.7 copy-start.1
  54.1 2.7 %copy-start = (f32[16,80,128]{2,1,0:T(8,128)}, f32[16,80,128]{2,1,0:T(8,128)S(1)}, u32[]{:S(2)}) copy-start(f32[16,80,128]{2,1,0:T(8,128)S(1)} %all_to_all.15.refs_2_.near) | copy-start | bytes 1966084
  54.1 5.6 %collective-permute-start.1 = (f32[16,80,128]{2,1,0:T(8,128)S(1)}, f32[16,80,128]{2,1,0:T(8,128)S(1)}, u32[]{:S(2)}, u32[]{:S(2)}) collective-permute-start(f32[16,80,128]{2,1,0:T(8,128)S(1)} %all_to_all.15.refs_2_.near), channel_id=1, source_target_pairs={{0,1},{1,0},{2,3},{3,2},{4,5},{5,4},{6,7},{7,6},{8,9},{9,8},{10,11... | collective-permute-start | bytes 1966088 | tf_op jit(solution)/shard_map/ppermute | solution.py:379
  59.7 0.8 %copy-start.2 = (f32[16,80,128]{2,1,0:T(8,128)}, f32[16,80,128]{2,1,0:T(8,128)S(1)}, u32[]{:S(2)}) copy-start(f32[16,80,128]{2,1,0:T(8,128)S(1)} %collective-permute-done.1.refs_2_.far) | copy-start | bytes 1966084
  62.6 12.0 %all-to-all-start.2 = ((f32[16,1,128]{2,1,0:T(1,128)}), f32[16,1,128]{2,1,0:T(1,128)S(1)}, u32[]{:S(2)}, u32[]{:S(2)}) async-start(f32[16,1,128]{2,1,0:T(1,128)} %share.1), calls=%async_computation.2 | async-start | bytes 16384 | tf_op jit(solution)/shard_map/all_to_all | solution.py:381

commit v2 on v1

v2 whole, which is shorter than its diff:
```python
import functools
import math

import jax
import jax.numpy as jnp
from jax import lax
from jax.experimental import pallas as pl
from jax.experimental.pallas import tpu as pltpu
from jax.sharding import PartitionSpec as P

GRID = 65536
BANDS = 1024
OBL_DEV = 1024
LANES = 128
HALF = BANDS // 2
A_LEN = 32
BLOCK = 512
F32 = jnp.float32
BF16 = jnp.bfloat16
I32 = jnp.int32


def iota(shape, dim):
    return lax.broadcasted_iota(I32, shape, dim)


def cos_sin(turns, log_grid):
    quarter_log = log_grid - 2
    quadrant = (turns + (1 << (quarter_log - 1))) >> quarter_log
    rest = turns - (quadrant << quarter_log)
    x = rest.astype(F32) * F32(2.0 * math.pi / (1 << log_grid))
    y = x * x
    sine = x * (1.0 + y * (-1.0 / 6 + y * (1.0 / 120 + y * (-1.0 / 5040 + y * (1.0 / 362880)))))
    cosine = 1.0 + y * (
        -0.5 + y * (1.0 / 24 + y * (-1.0 / 720 + y * (1.0 / 40320 - y * (1.0 / 3628800))))
    )
    odd = (quadrant & 1) == 1
    first = jnp.where(odd, cosine, sine)
    second = jnp.where(odd, sine, cosine)
    return (
        jnp.where(((quadrant + 1) & 2) == 2, -second, second),
        jnp.where((quadrant & 2) == 2, -first, first),
    )


def two_parts(value):
    high = value.astype(BF16).astype(F32)
    return high, value - high


def spectral_kernel(quantile, spec, mine, other, lhs, turn_cos, turn_sin, table, firsts, sums, lines, *grids):
    part = lax.axis_index("obl").astype(I32)
    core = part & 1
    scen = spec.shape[1]
    rows = 2 * scen
    shape = (A_LEN, LANES)
    freq = part * (A_LEN * LANES) + iota(shape, 0) * LANES + iota(shape, 1)
    zero = freq == 0
    half_cos, half_sin = cos_sin(freq, 17)
    v_im = jnp.where(zero, 0.0, 0.5 * half_cos / jnp.where(zero, 1.0, half_sin))
    v_re = jnp.where(zero, 0.0, 0.5)
    d_shape = (A_LEN, HALF)
    d_turn = ((part * A_LEN + iota(d_shape, 0)) * iota(d_shape, 1)) & (HALF - 1)
    d_cos, d_sin = cos_sin(d_turn, 9)
    dft = jnp.concatenate(
        [jnp.concatenate([d_cos, -d_sin], 1), jnp.concatenate([d_sin, d_cos], 1)], 0
    )
    d_high, d_low = two_parts(dft)
    d_high = d_high.astype(BF16)
    d_low = d_low.astype(BF16)
    table[...] = jnp.concatenate([d_high, d_high, d_low, d_low], 0)
    for c in range(scen):
        w_cos, w_sin = cos_sin((freq * (quantile[c] - 1)) & (GRID - 1), 16)
        u_re = v_re * w_cos - v_im * w_sin
        u_im = v_re * w_sin + v_im * w_cos
        for k in range(2):
            x_re = spec[0, c, pl.ds(k, A_LEN, stride=2), :]
            x_im = spec[1, c, pl.ds(k, A_LEN, stride=2), :]
            z_re = x_re * u_re - x_im * u_im
            z_im = x_re * u_im + x_im * u_re
            re_high, re_low = two_parts(z_re)
            im_high, im_low = two_parts(z_im)
            turned = jnp.concatenate([re_high, im_high, re_low, im_low], 0).T.astype(BF16)
            row = k * scen + c
            lhs[row * LANES : (row + 1) * LANES, :LANES] = turned
            lhs[row * LANES : (row + 1) * LANES, LANES:] = turned
            sums[row : row + 1, :] = jnp.sum(x_re * v_re - x_im * v_im, axis=0, keepdims=True)
            firsts[row : row + 1, :] = x_re[0:1, :]
    t_shape = (LANES, LANES)
    run_cos, run_sin = cos_sin(iota(t_shape, 0) * iota(t_shape, 1), 16)
    step_cos, step_sin = cos_sin(iota(t_shape, 0) * LANES, 16)
    for m in range(8):
        turn_cos[:, m * LANES : (m + 1) * LANES] = run_cos
        turn_sin[:, m * LANES : (m + 1) * LANES] = run_sin
        run_cos, run_sin = (
            run_cos * step_cos - run_sin * step_sin,
            run_sin * step_cos + run_cos * step_sin,
        )
    group = rows // len(grids)
    tiles = HALF // LANES
    for g, grid in enumerate(grids):
        grid[...] = jnp.dot(
            lhs[g * group * LANES : (g + 1) * group * LANES, :],
            table[...],
            preferred_element_type=F32,
        )
        for t in range(tiles):
            lane = t * LANES
            acc = [[None] * group for _ in range(2)]
            for b in range(LANES // 8):
                turn = [
                    (
                        turn_cos[b * 8 : (b + 1) * 8, h * HALF + lane : h * HALF + lane + LANES],
                        turn_sin[b * 8 : (b + 1) * 8, h * HALF + lane : h * HALF + lane + LANES],
                    )
                    for h in range(2)
                ]
                for r in range(group):
                    at = r * LANES + b * 8
                    g_re = grid[at : at + 8, lane : lane + LANES]
                    g_im = grid[at : at + 8, HALF + lane : HALF + lane + LANES]
                    for h in range(2):
                        term = g_re * turn[h][0] + g_im * turn[h][1]
                        acc[h][r] = term if acc[h][r] is None else acc[h][r] + term
            for h in range(2):
                for r in range(group):
                    at = ((h * tiles + t) * rows + g * group + r) * 8
                    lines[at : at + 8, :] = acc[h][r]
    total = jnp.sum(sums[...], axis=1, keepdims=True)
    at_zero = jnp.where(part == 0, firsts[:, 0:1], 0.0)
    lane_at = iota((1, LANES), 1)
    c_of = iota((scen, 1), 0)
    q_less = jnp.zeros((scen, 1), I32)
    for c in range(scen):
        q_less = jnp.where(c_of == c, quantile[c] - 1, q_less)
    for h in range(2):
        for t in range(tiles):
            for k in range(2):
                base = ((h * tiles + t) * rows + k * scen) * 8
                value = lines[pl.ds(base, scen, stride=8), :]
                for s in range(1, 8):
                    value = value + lines[pl.ds(base + s, scen, stride=8), :]
                size = (GRID - q_less + (h * HALF + t * LANES + lane_at)).astype(F32)
                here = slice(k * scen, (k + 1) * scen)
                value = (value + at_zero[here] * size - total[here]) * F32(1.0 / GRID)
                lines[pl.ds(base, scen), :] = value

    def send(h, to):
        for t in range(tiles):
            for k in range(2):
                base = ((h * tiles + t) * rows + k * scen) * 8
                to[t * rows + k * scen : t * rows + (k + 1) * scen, :] = lines[base : base + scen, :]

    @pl.when(core == 0)
    def _():
        send(0, mine)
        send(1, other)

    @pl.when(core == 1)
    def _():
        send(1, mine)
        send(0, other)


def spectral(quantile, spec):
    scen = spec.shape[1]
    rows = 2 * scen
    groups = 4
    smem = pl.BlockSpec(memory_space=pltpu.SMEM)
    vmem = pl.BlockSpec(memory_space=pltpu.VMEM)
    out = jax.ShapeDtypeStruct((HALF // LANES * rows, LANES), F32)
    return pl.pallas_call(
        spectral_kernel,
        out_shape=(out, out),
        in_specs=[smem, vmem],
        out_specs=(vmem, vmem),
        scratch_shapes=[
            pltpu.VMEM((rows * LANES, 2 * LANES), BF16),
            pltpu.VMEM((LANES, BANDS), F32),
            pltpu.VMEM((LANES, BANDS), F32),
            pltpu.VMEM((2 * LANES, 2 * HALF), BF16),
            pltpu.VMEM((rows, LANES), F32),
            pltpu.VMEM((rows, LANES), F32),
            pltpu.VMEM((BANDS // LANES * rows * 8, LANES), F32),
        ]
        + [pltpu.VMEM((rows // groups * LANES, 2 * HALF), F32)] * groups,
        compiler_params=pltpu.CompilerParams(vmem_limit_bytes=24 << 20),
        cost_estimate=pl.CostEstimate(flops=3_000_000_000, bytes_accessed=600_000, transcendentals=0),
        name="spectral",
    )(quantile, spec)


def slot_factor(bands, prob):
    return prob * bands.astype(F32) / 256.0


def band_weights_kernel(live, bands, prob, weights, mine, other, acc):
    sectors = weights.shape[0]
    acc[...] = jnp.zeros_like(acc)

    def block(n, _):
        at = pl.multiple_of(n * BLOCK, BLOCK)
        band = bands[:, pl.ds(at, BLOCK)]
        factor = slot_factor(band, prob[:, pl.ds(at, BLOCK)])
        alive = at + iota((1, BLOCK), 1) < live[0]
        factor = jnp.where(alive, factor, 0.0)
        index = band - 1
        low = index & 255
        high = index >> 8
        value = weights[:, pl.ds(at, BLOCK)].astype(F32) * factor
        v_high, v_low = two_parts(value)
        pieces = []
        for h in range(4):
            here = high == h
            pieces.append(jnp.where(here, v_high, 0.0).astype(BF16))
            pieces.append(jnp.where(here, v_low, 0.0).astype(BF16))
        left = jnp.concatenate(pieces, 0)
        hot = (iota((256, BLOCK), 0) == low).astype(F32).astype(BF16)
        acc[...] += lax.dot_general(
            left, hot, (((1,), (1,)), ((), ())), preferred_element_type=F32
        )
        return 0

    lax.fori_loop(0, (live[0] + BLOCK - 1) // BLOCK, block, 0)
    core = lax.axis_index("obl").astype(I32) & 1

    def send(half, to):
        for h in range(2):
            at = (2 * half + h) * 2 * sectors
            both = acc[at : at + sectors, :] + acc[at + sectors : at + 2 * sectors, :]
            for m in range(2):
                chunk = both[:, m * LANES : (m + 1) * LANES]
                to[pl.ds(2 * h + m, sectors, stride=4), :] = chunk

    @pl.when(core == 0)
    def _():
        send(0, mine)
        send(1, other)

    @pl.when(core == 1)
    def _():
        send(1, mine)
        send(0, other)


def band_weights(live, bands, prob, weights):
    sectors = weights.shape[0]
    smem = pl.BlockSpec(memory_space=pltpu.SMEM)
    vmem = pl.BlockSpec(memory_space=pltpu.VMEM)
    out = jax.ShapeDtypeStruct((sectors * HALF // LANES, LANES), F32)
    return pl.pallas_call(
        band_weights_kernel,
        out_shape=(out, out),
        in_specs=[smem, vmem, vmem, vmem],
        out_specs=(vmem, vmem),
        scratch_shapes=[pltpu.VMEM((8 * sectors, 256), F32)],
        compiler_params=pltpu.CompilerParams(vmem_limit_bytes=12 << 20),
        cost_estimate=pl.CostEstimate(flops=600_000_000, bytes_accessed=700_000, transcendentals=0),
        name="band_weights",
    )(live, bands, prob, weights)


def spread_kernel(mine, got, out):
    value = mine[...] + got[...]
    for n in range(out.shape[0]):
        out[n] = value


def spread(mine, got, copies):
    return pl.pallas_call(
        spread_kernel,
        out_shape=jax.ShapeDtypeStruct((copies, *mine.shape), F32),
        compiler_params=pltpu.CompilerParams(vmem_limit_bytes=4 << 20),
        name="spread",
    )(mine, got)


def join_kernel(parts, sums, got, out, own):
    value = parts[0]
    for n in range(1, parts.shape[0]):
        value = value + parts[n]
    rows = value.shape[0]
    own[...] = value
    for n in range(out.shape[0]):
        out[n, :rows, :] = value
        out[n, rows:, :] = sums[n] + got[n]


def join(parts, sums, got):
    peers, extra, lanes = sums.shape
    rows = parts.shape[1]
    return pl.pallas_call(
        join_kernel,
        out_shape=(
            jax.ShapeDtypeStruct((peers, rows + extra, lanes), F32),
            jax.ShapeDtypeStruct((rows, lanes), F32),
        ),
        compiler_params=pltpu.CompilerParams(vmem_limit_bytes=4 << 20),
        name="join",
    )(parts, sums, got)


def lookup_kernel(*refs, last):
    if last:
        live, tables, bands, prob, weights, before, out, lhs = refs
    else:
        live, tables, bands, weights, out, lhs = refs
    core = lax.axis_index("obl").astype(I32) & 1
    peers = tables.shape[0]
    rows = HALF // LANES
    each = 16
    count = peers * each
    sectors = weights.shape[0]
    scen = count // sectors
    for t in range(rows):
        value = tables[:, t * each : (t + 1) * each, :].reshape(count, LANES)
        high, low = two_parts(value)
        lhs[:count, t * LANES : (t + 1) * LANES] = high.astype(BF16)
        lhs[count:, t * LANES : (t + 1) * LANES] = low.astype(BF16)
    first = (core if not last else 1 - core) * HALF
    step = 2 * BLOCK
    steps = (live[0] + step - 1) // step

    def block(n, _):
        for part in range(2):
            at = pl.multiple_of(n * step + part * BLOCK, BLOCK)
            band = bands[:, pl.ds(at, BLOCK)]
            hot = (iota((HALF, BLOCK), 0) == band - 1 - first).astype(F32).astype(BF16)
            found = jnp.dot(lhs[...], hot, preferred_element_type=F32)
            weight = weights[:, pl.ds(at, BLOCK)].astype(F32)
            acc = jnp.zeros((scen, BLOCK), F32)
            for k in range(sectors):
                entry = found[k * scen : (k + 1) * scen] + found[count + k * scen : count + (k + 1) * scen]
                acc = acc + entry * weight[k : k + 1, :]
            if last:
                factor = slot_factor(band, prob[:, pl.ds(at, BLOCK)])
                alive = at + iota((1, BLOCK), 1) < live[0]
                acc = jnp.where(alive, (acc + before[:, pl.ds(at, BLOCK)]) * factor, 0.0)
            out[:, pl.ds(at, BLOCK)] = acc
        return 0

    lax.fori_loop(0, steps, block, 0)
    if last:

        def empty(n, _):
            at = pl.multiple_of(n * step, step)
            out[:, pl.ds(at, step)] = jnp.zeros((out.shape[0], step), F32)
            return 0

        lax.fori_loop(steps, out.shape[1] // step, empty, 0)


def lookup(live, tables, bands, prob, weights, before):
    last = before is not None
    slots = bands.shape[1]
    sectors = weights.shape[0]
    scen = tables.shape[0] * 16 // sectors
    smem = pl.BlockSpec(memory_space=pltpu.SMEM)
    vmem = pl.BlockSpec(memory_space=pltpu.VMEM)
    args = [live, tables, bands] + ([prob] if last else []) + [weights] + ([before] if last else [])
    return pl.pallas_call(
        functools.partial(lookup_kernel, last=last),
        out_shape=jax.ShapeDtypeStruct((scen, slots), F32),
        in_specs=[smem] + [vmem] * (len(args) - 1),
        out_specs=vmem,
        scratch_shapes=[pltpu.VMEM((tables.shape[0] * 32, HALF), BF16)],
        compiler_params=pltpu.CompilerParams(vmem_limit_bytes=24 << 20),
        cost_estimate=pl.CostEstimate(flops=4_300_000_000, bytes_accessed=1_000_000, transcendentals=0),
        name="lookup_last" if last else "lookup_first",
    )(*args)


def share_kernel(own, near, out):
    rows = own.shape[0]
    sums = near[0, rows:, :]
    for n in range(1, near.shape[0]):
        sums = sums + near[n, rows:, :]
    acc = [jnp.zeros((8, LANES), F32) for _ in range(2)]
    for t in range(4):
        for k in range(2):
            at = t * 16 + k * 8
            acc[k] = acc[k] + own[at : at + 8, :] * sums[k * 4 + t : k * 4 + t + 1, :]
    both = jnp.concatenate(acc + [jnp.zeros((LANES - 16, LANES), F32)], 0).T
    line = jnp.sum(both, axis=0, keepdims=True)
    for n in range(out.shape[0]):
        out[n] = line


def share(own, near, copies):
    return pl.pallas_call(
        share_kernel,
        out_shape=jax.ShapeDtypeStruct((copies, 1, LANES), F32),
        compiler_params=pltpu.CompilerParams(vmem_limit_bytes=4 << 20),
        cost_estimate=pl.CostEstimate(flops=1_000_000, bytes_accessed=100_000, transcendentals=0),
        name="share",
    )(own, near)


def total_kernel(shares, out, *, scale):
    line = shares[0]
    for n in range(1, shares.shape[0]):
        line = line + shares[n]
    line = line * F32(scale)
    out[0:1, :] = line[:, :8]
    out[1:2, :] = line[:, 8:16]


def total_of(shares, scale):
    return pl.pallas_call(
        functools.partial(total_kernel, scale=scale),
        out_shape=jax.ShapeDtypeStruct((2, 8), F32),
        compiler_params=pltpu.CompilerParams(vmem_limit_bytes=4 << 20),
        name="total",
    )(shares)


def on_device(spectrum, quantile_index, bands, default_prob, weights, live_rows):
    scen, sec_local = spectrum.shape[1], spectrum.shape[2]
    n_obl = lax.axis_size("obl")
    n_sector = lax.axis_size("sector")
    live = live_rows.reshape(1)
    spec = spectrum.reshape(2, scen, sec_local, A_LEN, LANES).transpose(0, 1, 3, 2, 4)
    spec = spec.reshape(2, scen, A_LEN * sec_local, LANES)
    bands = bands[None, :]
    prob = default_prob[None, :]
    swap = [(n, n ^ 1) for n in range(n_obl)]
    same_core = [[n for n in range(n_obl) if n % 2 == c] for c in range(2)]

    mine, other = spectral(quantile_index, spec)
    got = lax.ppermute(other, "obl", swap)
    copies = spread(mine, got, n_obl // 2)
    parts = lax.all_to_all(copies, "obl", 0, 0, axis_index_groups=same_core, tiled=True)
    sums, other_sums = band_weights(live, bands, prob, weights)
    got_sums = lax.ppermute(other_sums, "obl", swap)
    each = (n_sector, sums.shape[0] // n_sector, LANES)
    joined, own = join(parts, sums.reshape(each), got_sums.reshape(each))
    near = lax.all_to_all(joined, "sector", 0, 0, tiled=True)
    far = lax.ppermute(near, "obl", swap)
    shares = lax.all_to_all(share(own, near, n_obl), "obl", 0, 0, tiled=True)
    before = lookup(live, near, bands, prob, weights, None)
    contrib = lookup(live, far, bands, prob, weights, before)
    total = total_of(shares, sec_local * n_sector / (OBL_DEV * n_sector * n_obl)).T
    return contrib, total


def solution(mesh):
    in_specs = (
        P(None, None, "sector", "obl"),
        P(),
        P(("sector", "obl")),
        P(("sector", "obl")),
        P(None, ("sector", "obl")),
        P("sector", "obl"),
    )
    out_specs = (P(None, ("sector", "obl")), P(None, "sector"))
    return jax.shard_map(
        on_device, mesh=mesh, in_specs=in_specs, out_specs=out_specs, check_vma=False
    )
```

time: 75.4 us -> 61.9 us (0.82)
  Pallas kernels: 22 us -> 8.39 us
  waiting for transfers between devices: 13.3 us -> 16.1 us
  local copies, waits for them, and re-layouts: 2.8 us -> 1.7 us
  blocking collectives: 18 us -> 17.1 us
    pallas_call x3 -> x4, Pallas kernels: 12.6 us -> 4.65 us  [the longest x1 3.3 us: spectral(): pl.pallas_call(spectral_kernel, out_shape=(out, out), in_specs=[smem, vme...]
    pallas_call x2, Pallas kernels: 5.86 us -> 2.28 us  [lookup(): pl.pallas_call(functools.partial(lookup_kernel, last=last), out_shape=jax...]
    all_to_all x1, waiting for transfers between devices: 4.08 us -> 6.08 us  [on_device(): shares = lax.all_to_all(share(own, near, n_obl), 'obl', 0, 0, tiled=True)]
    all_to_all x1, starting transfers between devices: 4.9 us -> 3.37 us  [on_device(): shares = lax.all_to_all(share(own, near, n_obl), 'obl', 0, 0, tiled=True)]
    pallas_call x1, Pallas kernels: 2.02 us -> 0.73 us  [share(): pl.pallas_call(share_kernel, out_shape=jax.ShapeDtypeStruct((copies, 1, L...]
    ppermute x0 -> x1, waiting for transfers between devices: none -> 0.9 us  [on_device(): got_sums = lax.ppermute(other_sums, 'obl', swap)]
    all_to_all x1, blocking collectives: 18 us -> 17.1 us  [on_device(): near = lax.all_to_all(joined, 'sector', 0, 0, tiled=True)]
    pallas_call x1, Pallas kernels: 1.49 us -> 0.73 us  [spread(): pl.pallas_call(spread_kernel, out_shape=jax.ShapeDtypeStruct((copies, *mi...]
  transfers between devices with their start and end apart: 4 -> 5, of which waited for: 3 -> 4; matrix products, arithmetic and copies ran while one was open for 0% -> 0% of each run, Pallas kernels for 11% -> 5%
where the time goes in v2:
time: 61.9 us; the launch traced here: 61.4 us
  blocking collectives  17.1 us (28%)
  starting transfers between devices  16.7 us (27%)
  waiting for transfers between devices  16.1 us (26%)
  Pallas kernels  8.39 us (14%)
  local copies, waits for them, and re-layouts  1.7 us (3%)
  between operations  1.36 us (2%)
    all_to_all x1, blocking collectives, on_device(): near = lax.all_to_all(joined, 'sector', 0, 0, tiled=True)  17.1 us
    all_to_all x1, waiting for transfers between devices, on_device(): lax.all_to_all(copies, 'obl', 0, 0, axis_index_groups=same_core, tiled=True)  8.26 us
    all_to_all x1, starting transfers between devices, on_device(): lax.all_to_all(copies, 'obl', 0, 0, axis_index_groups=same_core, tiled=True)  6.61 us
    all_to_all x1, waiting for transfers between devices, on_device(): shares = lax.all_to_all(share(own, near, n_obl), 'obl', 0, 0, tiled=True)  6.08 us
    all_to_all x1, starting transfers between devices, on_device(): shares = lax.all_to_all(share(own, near, n_obl), 'obl', 0, 0, tiled=True)  3.37 us
    pallas_call x1, Pallas kernels, spectral(): pl.pallas_call(spectral_kernel, out_shape=(out, out), in_specs=[smem, vme...  3.3 us
    ppermute x1, starting transfers between devices, on_device(): got = lax.ppermute(other, 'obl', swap)  3.29 us
    ppermute x1, starting transfers between devices, on_device(): far = lax.ppermute(near, 'obl', swap)  2.72 us
  transfers between devices with their start and end apart: 5, of which 4 were waited for; matrix products, arithmetic and copies ran while one was open for 0% of the time, Pallas kernels for 5%

profile of v2, /device:TPU:1, one launch (start us, length us, event | category | flops | bytes accessed | tf_op | source)
XLA Modules:
  0.0 61.4 jit_solution(1107013617014285163)
XLA Ops:
  0.6 0.0 copy-start.4
  0.6 0.6 %copy-done.4 = s32[8]{0:T(128)S(1)} copy-done((s32[8]{0:T(128)S(1)}, s32[8]{0:T(128)}, u32[]{:S(2)}) %copy-start.4) | copy-done | bytes 56
  1.3 1.0 %copy-done = f32[2,8,2,4096]{3,2,1,0:T(2,128)S(1)} copy-done((f32[2,8,2,4096]{3,2,1,0:T(2,128)S(1)}, f32[2,8,2,4096]{3,2,1,0:T(2,128)}, u32[]{:S(2)}) %copy-start) | copy-done | bytes 524312
  2.3 3.3 %spectral.1 = (f32[64,128]{1,0:T(8,128)S(1)}, f32[64,128]{1,0:T(8,128)S(1)}) custom-call(s32[8]{0:T(128)S(1)} %copy-done.4, f32[2,8,64,128]{3,2,1,0:T(8,128)S(1)} %bitcast.16), custom_call_target="tpu_custom_call" | custom-call | flops 3000000000 | bytes 600000 | tf_op jit(solution)/shard_map/spectral/pallas_call | solution.py:172
  5.6 0.0 copy-start.1
  5.7 3.3 %collective-permute-start = (f32[64,128]{1,0:T(8,128)S(1)}, f32[64,128]{1,0:T(8,128)S(1)}, u32[]{:S(2)}, u32[]{:S(2)}) collective-permute-start(f32[64,128]{1,0:T(8,128)S(1)} %get-tuple-element.9), channel_id=1, source_target_pairs={{0,1},{1,0},{2,3},{3,2},{4,5},{5,4},{6,7},{7,6},{8,9},{9,8},{10,11... | collective-permute-start | bytes 98312 | tf_op jit(solution)/shard_map/ppermute | solution.py:430
  8.9 0.9 %collective-permute-done.got = f32[64,128]{1,0:T(8,128)S(1)} collective-permute-done((f32[64,128]{1,0:T(8,128)S(1)}, f32[64,128]{1,0:T(8,128)S(1)}, u32[]{:S(2)}, u32[]{:S(2)}) %collective-permute-start) | collective-permute-done | bytes 32800 | tf_op jit(solution)/shard_map/ppermute | solution.py:430
  9.8 0.7 %spread.1 = f32[8,64,128]{2,1,0:T(8,128)} custom-call(f32[64,128]{1,0:T(8,128)S(1)} %get-tuple-element.8.mine, f32[64,128]{1,0:T(8,128)S(1)} %collective-permute-done.got), custom_call_target="tpu_custom_call" | custom-call | tf_op jit(solution)/shard_map/spread/pallas_call | solution.py:270
  10.5 6.6 %all-to-all-start = ((f32[8,64,128]{2,1,0:T(8,128)}), f32[8,64,128]{2,1,0:T(8,128)S(1)}, u32[]{:S(2)}, u32[]{:S(2)}) async-start(f32[8,64,128]{2,1,0:T(8,128)} %spread.1), calls=%async_computation | async-start | bytes 524288 | tf_op jit(solution)/shard_map/all_to_all | solution.py:432
  17.8 0.0 copy-done.1
  17.8 0.0 copy-done.2
  17.8 0.7 %band_weights.1 = (f32[128,128]{1,0:T(8,128)S(1)}, f32[128,128]{1,0:T(8,128)S(1)}) custom-call(s32[1]{0:T(128)} %bitcast.11.live, s32[1,4096]{1,0:T(1,128)S(1)} %bitcast.17, f32[1,4096]{1,0:T(1,128)S(1)} %bitcast.20, s32[32,4096]{1,0:T(8,128)S(1)} %copy-done.1), custom_call_target="tpu_custom_call" | custom-call | flops 600000000 | bytes 700000 | tf_op jit(solution)/shard_map/band_weights/pallas_call | solution.py:251
  18.5 0.7 %collective-permute-start.1 = (f32[128,128]{1,0:T(8,128)S(1)}, f32[128,128]{1,0:T(8,128)S(1)}, u32[]{:S(2)}, u32[]{:S(2)}) collective-permute-start(f32[128,128]{1,0:T(8,128)S(1)} %get-tuple-element.11), channel_id=1, source_target_pairs={{0,1},{1,0},{2,3},{3,2},{4,5},{5,4},{6,7},{7,6},{8,9},{9,8},{10,11... | collective-permute-start | bytes 196616 | tf_op jit(solution)/shard_map/ppermute | solution.py:434
  19.2 0.9 %collective-permute-done.1 = f32[128,128]{1,0:T(8,128)S(1)} collective-permute-done((f32[128,128]{1,0:T(8,128)S(1)}, f32[128,128]{1,0:T(8,128)S(1)}, u32[]{:S(2)}, u32[]{:S(2)}) %collective-permute-start.1) | collective-permute-done | bytes 65568 | tf_op jit(solution)/shard_map/ppermute | solution.py:434
  20.1 8.3 %all-to-all-done.parts = f32[8,64,128]{2,1,0:T(8,128)S(1)} async-done(((f32[8,64,128]{2,1,0:T(8,128)}), f32[8,64,128]{2,1,0:T(8,128)S(1)}, u32[]{:S(2)}, u32[]{:S(2)}) %all-to-all-start) | async-done | bytes 262176 | tf_op jit(solution)/shard_map/all_to_all | solution.py:432
  28.4 17.1 %all_to_all.15.refs_1_.near = f32[16,72,128]{2,1,0:T(8,128)S(1)} all-to-all(f32[16,72,128]{2,1,0:T(8,128)S(1)} %get-tuple-element.12), channel_id=1, replica_groups=mesh['sector'=16,'obl'=16] {'sector'}, dimensions={0} | all-to-all | bytes 1179648 | tf_op jit(solution)/shard_map/all_to_all | solution.py:437
  45.5 2.7 %collective-permute-start.2 = (f32[16,72,128]{2,1,0:T(8,128)S(1)}, f32[16,72,128]{2,1,0:T(8,128)S(1)}, u32[]{:S(2)}, u32[]{:S(2)}) collective-permute-start(f32[16,72,128]{2,1,0:T(8,128)S(1)} %all_to_all.15.refs_1_.near), channel_id=1, source_target_pairs={{0,1},{1,0},{2,3},{3,2},{4,5},{5,4},{6,7},{7,6},{8,9},{9,8},{10,11... | collective-permute-start | bytes 1769480 | tf_op jit(solution)/shard_map/ppermute | solution.py:438
  48.2 0.7 %share.1 = f32[16,1,128]{2,1,0:T(1,128)} custom-call(f32[64,128]{1,0:T(8,128)S(1)} %get-tuple-element.13.own, f32[16,72,128]{2,1,0:T(8,128)S(1)} %all_to_all.15.refs_1_.near), custom_call_target="tpu_custom_call" | custom-call | flops 1000000 | bytes 100000 | tf_op jit(solution)/shard_map/share/pallas_call | solution.py:390
  49.0 3.4 %all-to-all-start.2 = ((f32[16,1,128]{2,1,0:T(1,128)}), f32[16,1,128]{2,1,0:T(1,128)S(1)}, u32[]{:S(2)}, u32[]{:S(2)}) async-start(f32[16,1,128]{2,1,0:T(1,128)} %share.1), calls=%async_computation.2 | async-start | bytes 16384 | tf_op jit(solution)/shard_map/all_to_all | solution.py:439
  52.3 0.8 %lookup_first.1.refs_5_ = f32[8,4096]{1,0:T(8,128)S(1)} custom-call(s32[1]{0:T(128)} %bitcast.12.refs_0_, f32[16,72,128]{2,1,0:T(8,128)S(1)} %all_to_all.15.refs_1_.near, s32[1,4096]{1,0:T(1,128)S(1)} %bitcast.18, s32[32,4096]{1,0:T(8,128)S(1)} %copy-done.1), custom_call_target="tpu_custom_call" | custom-call | flops 4300000256 | bytes 1000000 | tf_op jit(solution)/shard_map/lookup_first/pallas_call | solution.py:361
  53.1 6.1 %all-to-all-done.2.shares = f32[16,1,128]{2,1,0:T(1,128)S(1)} async-done(((f32[16,1,128]{2,1,0:T(1,128)}), f32[16,1,128]{2,1,0:T(1,128)S(1)}, u32[]{:S(2)}, u32[]{:S(2)}) %all-to-all-start.2) | async-done | bytes 8224 | tf_op jit(solution)/shard_map/all_to_all | solution.py:439
  59.2 0.6 %total.1 = f32[2,8]{1,0:T(2,128)} custom-call(f32[16,1,128]{2,1,0:T(1,128)S(1)} %all-to-all-done.2.shares), custom_call_target="tpu_custom_call" | custom-call | tf_op jit(solution)/shard_map/total/pallas_call | solution.py:409
  59.9 0.0 collective-permute-done.2.refs_1_
  59.9 1.5 %lookup_last.1 = f32[8,4096]{1,0:T(8,128)} custom-call(s32[1]{0:T(128)} %bitcast.13.refs_0_, f32[16,72,128]{2,1,0:T(8,128)S(1)} %collective-permute-done.2.refs_1_, s32[1,4096]{1,0:T(1,128)S(1)} %bitcast.19, f32[1,4096]{1,0:T(1,128)S(1)} %bitcast.21, s32[32,4096]{1,0:T(8,128)S(1)} %copy-done.1, f32[8,4096]{1,0:T(8,128)S(1)} %lookup_first.1.refs_5_), custom_call_target="tpu_custom_call" | custom-call | flops 4300000256 | bytes 1000000 | tf_op jit(solution)/shard_map/lookup_last/pallas_call | solution.py:361
  (5 shorter events, 0.1 us)
Async XLA Ops:
  0.6 0.7 %copy-start.4 = (s32[8]{0:T(128)S(1)}, s32[8]{0:T(128)}, u32[]{:S(2)}) copy-start(s32[8]{0:T(128)} %quantile.1) | copy-start | bytes 100
  1.3 1.0 %copy-start = (f32[2,8,2,4096]{3,2,1,0:T(2,128)S(1)}, f32[2,8,2,4096]{3,2,1,0:T(2,128)}, u32[]{:S(2)}) copy-start(f32[2,8,2,4096]{3,2,1,0:T(2,128)} %param.6) | copy-start | bytes 1572868
  5.6 12.2 %copy-start.1 = (s32[32,4096]{1,0:T(8,128)S(1)}, s32[32,4096]{1,0:T(8,128)}, u32[]{:S(2)}) copy-start(s32[32,4096]{1,0:T(8,128)} %refs_4_.1) | copy-start | bytes 1572868
  5.7 4.2 %collective-permute-start = (f32[64,128]{1,0:T(8,128)S(1)}, f32[64,128]{1,0:T(8,128)S(1)}, u32[]{:S(2)}, u32[]{:S(2)}) collective-permute-start(f32[64,128]{1,0:T(8,128)S(1)} %get-tuple-element.9), channel_id=1, source_target_pairs={{0,1},{1,0},{2,3},{3,2},{4,5},{5,4},{6,7},{7,6},{8,9},{9,8},{10,11... | collective-permute-start | bytes 98312 | tf_op jit(solution)/shard_map/ppermute | solution.py:430
  10.5 7.3 %copy-start.2 = (s32[4096]{0:T(1024)S(1)}, s32[4096]{0:T(1024)}, u32[]{:S(2)}) copy-start(s32[4096]{0:T(1024)} %param.8) | copy-start | bytes 49156
  10.5 7.3 %copy-start.3 = (f32[4096]{0:T(1024)S(1)}, f32[4096]{0:T(1024)}, u32[]{:S(2)}) copy-start(f32[4096]{0:T(1024)} %param.9) | copy-start | bytes 49156
  10.5 17.8 %all-to-all-start = ((f32[8,64,128]{2,1,0:T(8,128)}), f32[8,64,128]{2,1,0:T(8,128)S(1)}, u32[]{:S(2)}, u32[]{:S(2)}) async-start(f32[8,64,128]{2,1,0:T(8,128)} %spread.1), calls=%async_computation | async-start | bytes 524288 | tf_op jit(solution)/shard_map/all_to_all | solution.py:432
  18.5 1.6 %collective-permute-start.1 = (f32[128,128]{1,0:T(8,128)S(1)}, f32[128,128]{1,0:T(8,128)S(1)}, u32[]{:S(2)}, u32[]{:S(2)}) collective-permute-start(f32[128,128]{1,0:T(8,128)S(1)} %get-tuple-element.11), channel_id=1, source_target_pairs={{0,1},{1,0},{2,3},{3,2},{4,5},{5,4},{6,7},{7,6},{8,9},{9,8},{10,11... | collective-permute-start | bytes 196616 | tf_op jit(solution)/shard_map/ppermute | solution.py:434
  45.5 14.4 %collective-permute-start.2 = (f32[16,72,128]{2,1,0:T(8,128)S(1)}, f32[16,72,128]{2,1,0:T(8,128)S(1)}, u32[]{:S(2)}, u32[]{:S(2)}) collective-permute-start(f32[16,72,128]{2,1,0:T(8,128)S(1)} %all_to_all.15.refs_1_.near), channel_id=1, source_target_pairs={{0,1},{1,0},{2,3},{3,2},{4,5},{5,4},{6,7},{7,6},{8,9},{9,8},{10,11... | collective-permute-start | bytes 1769480 | tf_op jit(solution)/shard_map/ppermute | solution.py:438
  49.0 10.3 %all-to-all-start.2 = ((f32[16,1,128]{2,1,0:T(1,128)}), f32[16,1,128]{2,1,0:T(1,128)S(1)}, u32[]{:S(2)}, u32[]{:S(2)}) async-start(f32[16,1,128]{2,1,0:T(1,128)} %share.1), calls=%async_computation.2 | async-start | bytes 16384 | tf_op jit(solution)/shard_map/all_to_all | solution.py:439

commit v3 on v2

--- a/solution.py
+++ b/solution.py
@@ -7,6 +7,7 @@
 from jax.experimental import pallas as pl
 from jax.experimental.pallas import tpu as pltpu
 from jax.sharding import PartitionSpec as P
+
 
 GRID = 65536
 BANDS = 1024
@@ -48,11 +49,17 @@
     return high, value - high
 
 
-def spectral_kernel(quantile, spec, mine, other, lhs, turn_cos, turn_sin, table, firsts, sums, lines, *grids):
+def spectral_kernel(quantile_hbm, spec_hbm, mine, other, quantile, spec, sems, lhs, turn_cos, turn_sin, table, firsts, sums, lines, *grids):
     part = lax.axis_index("obl").astype(I32)
     core = part & 1
     scen = spec.shape[1]
     rows = 2 * scen
+    copies = [
+        pltpu.make_async_copy(quantile_hbm, quantile, sems.at[0]),
+        pltpu.make_async_copy(spec_hbm, spec, sems.at[1]),
+    ]
+    for copy in copies:
+        copy.start()
     shape = (A_LEN, LANES)
     freq = part * (A_LEN * LANES) + iota(shape, 0) * LANES + iota(shape, 1)
     zero = freq == 0
@@ -69,6 +76,18 @@
     d_high = d_high.astype(BF16)
     d_low = d_low.astype(BF16)
     table[...] = jnp.concatenate([d_high, d_high, d_low, d_low], 0)
+    t_shape = (LANES, LANES)
+    run_cos, run_sin = cos_sin(iota(t_shape, 0) * iota(t_shape, 1), 16)
+    step_cos, step_sin = cos_sin(iota(t_shape, 0) * LANES, 16)
+    for m in range(8):
+        turn_cos[:, m * LANES : (m + 1) * LANES] = run_cos
+        turn_sin[:, m * LANES : (m + 1) * LANES] = run_sin
+        run_cos, run_sin = (
+            run_cos * step_cos - run_sin * step_sin,
+            run_sin * step_cos + run_cos * step_sin,
+        )
+    for copy in copies:
+        copy.wait()
     for c in range(scen):
         w_cos, w_sin = cos_sin((freq * (quantile[c] - 1)) & (GRID - 1), 16)
         u_re = v_re * w_cos - v_im * w_sin
@@ -86,16 +105,6 @@
             lhs[row * LANES : (row + 1) * LANES, LANES:] = turned
             sums[row : row + 1, :] = jnp.sum(x_re * v_re - x_im * v_im, axis=0, keepdims=True)
             firsts[row : row + 1, :] = x_re[0:1, :]
-    t_shape = (LANES, LANES)
-    run_cos, run_sin = cos_sin(iota(t_shape, 0) * iota(t_shape, 1), 16)
-    step_cos, step_sin = cos_sin(iota(t_shape, 0) * LANES, 16)
-    for m in range(8):
-        turn_cos[:, m * LANES : (m + 1) * LANES] = run_cos
-        turn_sin[:, m * LANES : (m + 1) * LANES] = run_sin
-        run_cos, run_sin = (
-            run_cos * step_cos - run_sin * step_sin,
-            run_sin * step_cos + run_cos * step_sin,
-        )
     group = rows // len(grids)
     tiles = HALF // LANES
     for g, grid in enumerate(grids):
@@ -166,15 +175,18 @@
     scen = spec.shape[1]
     rows = 2 * scen
     groups = 4
-    smem = pl.BlockSpec(memory_space=pltpu.SMEM)
+    hbm = pl.BlockSpec(memory_space=pltpu.HBM)
     vmem = pl.BlockSpec(memory_space=pltpu.VMEM)
     out = jax.ShapeDtypeStruct((HALF // LANES * rows, LANES), F32)
     return pl.pallas_call(
         spectral_kernel,
         out_shape=(out, out),
-        in_specs=[smem, vmem],
+        in_specs=[hbm, hbm],
         out_specs=(vmem, vmem),
         scratch_shapes=[
+            pltpu.SMEM(quantile.shape, I32),
+            pltpu.VMEM(spec.shape, F32),
+            pltpu.SemaphoreType.DMA((2,)),
             pltpu.VMEM((rows * LANES, 2 * LANES), BF16),
             pltpu.VMEM((LANES, BANDS), F32),
             pltpu.VMEM((LANES, BANDS), F32),
@@ -187,7 +199,10 @@
         compiler_params=pltpu.CompilerParams(vmem_limit_bytes=24 << 20),
         cost_estimate=pl.CostEstimate(flops=3_000_000_000, bytes_accessed=600_000, transcendentals=0),
         name="spectral",
-    )(quantile, spec)
+    )(
+        pltpu.with_memory_space_constraint(quantile, pltpu.HBM),
+        pltpu.with_memory_space_constraint(spec, pltpu.HBM),
+    )
 
 
 def slot_factor(bands, prob):
@@ -202,7 +217,7 @@
         at = pl.multiple_of(n * BLOCK, BLOCK)
         band = bands[:, pl.ds(at, BLOCK)]
         factor = slot_factor(band, prob[:, pl.ds(at, BLOCK)])
-        alive = at + iota((1, BLOCK), 1) < live[0]
+        alive = at + iota((1, BLOCK), 1) < live[0, 0]
         factor = jnp.where(alive, factor, 0.0)
         index = band - 1
         low = index & 255
@@ -221,7 +236,7 @@
         )
         return 0
 
-    lax.fori_loop(0, (live[0] + BLOCK - 1) // BLOCK, block, 0)
+    lax.fori_loop(0, (live[0, 0] + BLOCK - 1) // BLOCK, block, 0)
     core = lax.axis_index("obl").astype(I32) & 1
 
     def send(half, to):
@@ -260,16 +275,17 @@
     )(live, bands, prob, weights)
 
 
-def spread_kernel(mine, got, out):
+def spread_kernel(mine, got, out, *, parities):
     value = mine[...] + got[...]
-    for n in range(out.shape[0]):
-        out[n] = value
-
-
-def spread(mine, got, copies):
-    return pl.pallas_call(
-        spread_kernel,
-        out_shape=jax.ShapeDtypeStruct((copies, *mine.shape), F32),
+    rows = out.shape[1]
+    for n, parity in enumerate(parities):
+        out[n] = value[parity * rows : (parity + 1) * rows]
+
+
+def spread(mine, got, parities):
+    return pl.pallas_call(
+        functools.partial(spread_kernel, parities=parities),
+        out_shape=jax.ShapeDtypeStruct((len(parities), mine.shape[0] // 2, LANES), F32),
         compiler_params=pltpu.CompilerParams(vmem_limit_bytes=4 << 20),
         name="spread",
     )(mine, got)
@@ -302,30 +318,37 @@
 
 def lookup_kernel(*refs, last):
     if last:
-        live, tables, bands, prob, weights, before, out, lhs = refs
+        live, same, cross, bands, prob, weights, before, out, lhs = refs
     else:
-        live, tables, bands, weights, out, lhs = refs
-    core = lax.axis_index("obl").astype(I32) & 1
-    peers = tables.shape[0]
+        live, same, cross, bands, weights, out, lhs = refs
+    place = lax.axis_index("obl").astype(I32)
+    core = place & 1
+    parity = (place >> 1) & 1
+    peers = same.shape[0]
     rows = HALF // LANES
     each = 16
     count = peers * each
     sectors = weights.shape[0]
     scen = count // sectors
     for t in range(rows):
-        value = tables[:, t * each : (t + 1) * each, :].reshape(count, LANES)
+        side = same if t < 2 else cross
+        at = (t % 2) * each
+        value = side[:, at : at + each, :].reshape(count, LANES)
         high, low = two_parts(value)
         lhs[:count, t * LANES : (t + 1) * LANES] = high.astype(BF16)
         lhs[count:, t * LANES : (t + 1) * LANES] = low.astype(BF16)
-    first = (core if not last else 1 - core) * HALF
+    want = 1 - parity if last else parity
     step = 2 * BLOCK
-    steps = (live[0] + step - 1) // step
+    steps = (live[0, 0] + step - 1) // step
 
     def block(n, _):
         for part in range(2):
             at = pl.multiple_of(n * step + part * BLOCK, BLOCK)
             band = bands[:, pl.ds(at, BLOCK)]
-            hot = (iota((HALF, BLOCK), 0) == band - 1 - first).astype(F32).astype(BF16)
+            index = band - 1
+            column = (index & 255) + jnp.where((index >> 9) == core, 0, 256)
+            column = jnp.where(((index >> 8) & 1) == want, column, -1)
+            hot = (iota((HALF, BLOCK), 0) == column).astype(F32).astype(BF16)
             found = jnp.dot(lhs[...], hot, preferred_element_type=F32)
             weight = weights[:, pl.ds(at, BLOCK)].astype(F32)
             acc = jnp.zeros((scen, BLOCK), F32)
@@ -334,7 +357,7 @@
                 acc = acc + entry * weight[k : k + 1, :]
             if last:
                 factor = slot_factor(band, prob[:, pl.ds(at, BLOCK)])
-                alive = at + iota((1, BLOCK), 1) < live[0]
+                alive = at + iota((1, BLOCK), 1) < live[0, 0]
                 acc = jnp.where(alive, (acc + before[:, pl.ds(at, BLOCK)]) * factor, 0.0)
             out[:, pl.ds(at, BLOCK)] = acc
         return 0
@@ -350,50 +373,54 @@
         lax.fori_loop(steps, out.shape[1] // step, empty, 0)
 
 
-def lookup(live, tables, bands, prob, weights, before):
+def lookup(live, same, cross, bands, prob, weights, before):
     last = before is not None
     slots = bands.shape[1]
     sectors = weights.shape[0]
-    scen = tables.shape[0] * 16 // sectors
+    scen = same.shape[0] * 16 // sectors
     smem = pl.BlockSpec(memory_space=pltpu.SMEM)
     vmem = pl.BlockSpec(memory_space=pltpu.VMEM)
-    args = [live, tables, bands] + ([prob] if last else []) + [weights] + ([before] if last else [])
+    args = [live, same, cross, bands] + ([prob] if last else []) + [weights] + ([before] if last else [])
     return pl.pallas_call(
         functools.partial(lookup_kernel, last=last),
         out_shape=jax.ShapeDtypeStruct((scen, slots), F32),
         in_specs=[smem] + [vmem] * (len(args) - 1),
         out_specs=vmem,
-        scratch_shapes=[pltpu.VMEM((tables.shape[0] * 32, HALF), BF16)],
+        scratch_shapes=[pltpu.VMEM((same.shape[0] * 32, HALF), BF16)],
         compiler_params=pltpu.CompilerParams(vmem_limit_bytes=24 << 20),
         cost_estimate=pl.CostEstimate(flops=4_300_000_000, bytes_accessed=1_000_000, transcendentals=0),
         name="lookup_last" if last else "lookup_first",
     )(*args)
 
 
-def share_kernel(own, near, out):
+def share_kernel(own, across, near, out):
+    parity = (lax.axis_index("obl").astype(I32) >> 1) & 1
     rows = own.shape[0]
     sums = near[0, rows:, :]
     for n in range(1, near.shape[0]):
         sums = sums + near[n, rows:, :]
     acc = [jnp.zeros((8, LANES), F32) for _ in range(2)]
-    for t in range(4):
+    for t in range(2):
         for k in range(2):
             at = t * 16 + k * 8
-            acc[k] = acc[k] + own[at : at + 8, :] * sums[k * 4 + t : k * 4 + t + 1, :]
+            low = sums[k * 4 + t : k * 4 + t + 1, :]
+            high = sums[k * 4 + 2 + t : k * 4 + 3 + t, :]
+            acc[k] = acc[k] + own[at : at + 8, :] * jnp.where(parity == 0, low, high)
+            acc[k] = acc[k] + across[at : at + 8, :] * jnp.where(parity == 0, high, low)
     both = jnp.concatenate(acc + [jnp.zeros((LANES - 16, LANES), F32)], 0).T
     line = jnp.sum(both, axis=0, keepdims=True)
     for n in range(out.shape[0]):
         out[n] = line
 
 
-def share(own, near, copies):
+def share(own, across, near, copies):
     return pl.pallas_call(
         share_kernel,
         out_shape=jax.ShapeDtypeStruct((copies, 1, LANES), F32),
         compiler_params=pltpu.CompilerParams(vmem_limit_bytes=4 << 20),
         cost_estimate=pl.CostEstimate(flops=1_000_000, bytes_accessed=100_000, transcendentals=0),
         name="share",
-    )(own, near)
+    )(own, across, near)
 
 
 def total_kernel(shares, out, *, scale):
@@ -414,31 +441,37 @@
     )(shares)
 
 
-def on_device(spectrum, quantile_index, bands, default_prob, weights, live_rows):
+def contributions(spectrum, quantile_index, bands, default_prob, weights, live_rows):
     scen, sec_local = spectrum.shape[1], spectrum.shape[2]
     n_obl = lax.axis_size("obl")
     n_sector = lax.axis_size("sector")
-    live = live_rows.reshape(1)
+    live = live_rows
     spec = spectrum.reshape(2, scen, sec_local, A_LEN, LANES).transpose(0, 1, 3, 2, 4)
     spec = spec.reshape(2, scen, A_LEN * sec_local, LANES)
     bands = bands[None, :]
     prob = default_prob[None, :]
     swap = [(n, n ^ 1) for n in range(n_obl)]
-    same_core = [[n for n in range(n_obl) if n % 2 == c] for c in range(2)]
-
+    same_core = [[n for n in reversed(range(n_obl)) if n % 2 == c] for c in range(2)]
+
+    next_plane = [(n, n ^ 2) for n in range(n_obl)]
     mine, other = spectral(quantile_index, spec)
     got = lax.ppermute(other, "obl", swap)
-    copies = spread(mine, got, n_obl // 2)
+    copies = spread(mine, got, tuple(n >> 1 & 1 for n in same_core[0]))
     parts = lax.all_to_all(copies, "obl", 0, 0, axis_index_groups=same_core, tiled=True)
     sums, other_sums = band_weights(live, bands, prob, weights)
     got_sums = lax.ppermute(other_sums, "obl", swap)
     each = (n_sector, sums.shape[0] // n_sector, LANES)
     joined, own = join(parts, sums.reshape(each), got_sums.reshape(each))
+    across = lax.ppermute(own, "obl", next_plane)
     near = lax.all_to_all(joined, "sector", 0, 0, tiled=True)
-    far = lax.ppermute(near, "obl", swap)
-    shares = lax.all_to_all(share(own, near, n_obl), "obl", 0, 0, tiled=True)
-    before = lookup(live, near, bands, prob, weights, None)
-    contrib = lookup(live, far, bands, prob, weights, before)
+    tables = near[:, : own.shape[0]]
+    tables_across = lax.ppermute(tables, "obl", next_plane)
+    tables_beside = lax.ppermute(tables, "obl", swap)
+    shares = share(own, across, near, n_obl)
+    shares = lax.all_to_all(shares, "obl", 0, 0, tiled=True)
+    before = lookup(live, tables, tables_beside, bands, prob, weights, None)
+    tables_corner = lax.ppermute(tables_across, "obl", swap)
+    contrib = lookup(live, tables_across, tables_corner, bands, prob, weights, before)
     total = total_of(shares, sec_local * n_sector / (OBL_DEV * n_sector * n_obl)).T
     return contrib, total
 
@@ -454,5 +487,5 @@
     )
     out_specs = (P(None, ("sector", "obl")), P(None, "sector"))
     return jax.shard_map(
-        on_device, mesh=mesh, in_specs=in_specs, out_specs=out_specs, check_vma=False
-    )
+        contributions, mesh=mesh, in_specs=in_specs, out_specs=out_specs, check_vma=False
+    )

time: 61.9 us -> 62.2 us (level)
  blocking collectives: 17.1 us -> 28.5 us
  waiting for transfers between devices: 16.1 us -> 6.8 us
  local copies, waits for them, and re-layouts: 1.7 us -> 0.03 us
    all_to_all x2 -> x1, waiting for transfers between devices: 14.3 us -> 1.65 us  [contributions(): lax.all_to_all(copies, 'obl', 0, 0, axis_index_groups=same_core, tiled=True)]
    all_to_all x1 -> x2, blocking collectives: 17.1 us -> 28.5 us  [the longest x1 14.4 us: contributions(): near = lax.all_to_all(joined, 'sector', 0, 0, tiled=True)]
    ppermute x3 -> x6, waiting for transfers between devices: 1.76 us -> 5.15 us  [the longest x1 3.03 us: contributions(): across = lax.ppermute(own, 'obl', next_plane)]
    ppermute x3 -> x6, starting transfers between devices: 6.72 us -> 9.63 us  [the longest x1 3.29 us: contributions(): got = lax.ppermute(other, 'obl', swap)]
    all_to_all x2 -> x1, starting transfers between devices: 9.98 us -> 7.32 us  [contributions(): lax.all_to_all(copies, 'obl', 0, 0, axis_index_groups=same_core, tiled=True)]
    unnamed x10 -> x6, local copies, waits for them, and re-layouts: 1.7 us -> 0.01 us
  transfers between devices with their start and end apart: 5 -> 7, of which waited for: 4 -> 5; matrix products, arithmetic and copies ran while one was open for 0% -> 0% of each run, Pallas kernels for 5% -> 4%
where the time goes in v3:
time: 62.2 us; the launch traced here: 61.6 us
  blocking collectives  28.5 us (46%)
  starting transfers between devices  16.9 us (27%)
  Pallas kernels  7.99 us (13%)
  waiting for transfers between devices  6.8 us (11%)
  between operations  1.36 us (2%)
    all_to_all x1, blocking collectives, contributions(): near = lax.all_to_all(joined, 'sector', 0, 0, tiled=True)  14.4 us
    all_to_all x1, blocking collectives, contributions(): shares = lax.all_to_all(shares, 'obl', 0, 0, tiled=True)  14.1 us
    all_to_all x1, starting transfers between devices, contributions(): lax.all_to_all(copies, 'obl', 0, 0, axis_index_groups=same_core, tiled=True)  7.32 us
    pallas_call x1, Pallas kernels, spectral(): pl.pallas_call(spectral_kernel, out_shape=(out, out), in_specs=[hbm, hbm]...  3.59 us
    ppermute x1, starting transfers between devices, contributions(): got = lax.ppermute(other, 'obl', swap)  3.29 us
    ppermute x1, waiting for transfers between devices, contributions(): across = lax.ppermute(own, 'obl', next_plane)  3.03 us
    ppermute x1, starting transfers between devices, contributions(): tables_beside = lax.ppermute(tables, 'obl', swap)  2.51 us
    pallas_call x2, Pallas kernels, lookup(): pl.pallas_call(functools.partial(lookup_kernel, last=last), out_shape=jax...  2.28 us
  transfers between devices with their start and end apart: 7, of which 5 were waited for; matrix products, arithmetic and copies ran while one was open for 0% of the time, Pallas kernels for 4%

profile of v3, /device:TPU:1, one launch (start us, length us, event | category | flops | bytes accessed | tf_op | source)
XLA Modules:
  0.0 61.6 jit_solution(16071501479552988346)
XLA Ops:
  0.6 0.0 copy-start
  0.6 3.6 %spectral.1 = (f32[64,128]{1,0:T(8,128)S(1)}, f32[64,128]{1,0:T(8,128)S(1)}) custom-call(s32[8]{0:T(128)} %quantile_hbm.1, f32[2,8,64,128]{3,2,1,0:T(8,128)} %bitcast.18), custom_call_target="tpu_custom_call" | custom-call | flops 3000000000 | bytes 600000 | tf_op jit(solution)/shard_map/spectral/pallas_call | solution.py:181
  4.2 3.3 %collective-permute-start = (f32[64,128]{1,0:T(8,128)S(1)}, f32[64,128]{1,0:T(8,128)S(1)}, u32[]{:S(2)}, u32[]{:S(2)}) collective-permute-start(f32[64,128]{1,0:T(8,128)S(1)} %get-tuple-element.9), channel_id=1, source_target_pairs={{0,1},{1,0},{2,3},{3,2},{4,5},{5,4},{6,7},{7,6},{8,9},{9,8},{10,11... | collective-permute-start | bytes 98312 | tf_op jit(solution)/shard_map/ppermute | solution.py:458
  7.5 0.9 %collective-permute-done.got = f32[64,128]{1,0:T(8,128)S(1)} collective-permute-done((f32[64,128]{1,0:T(8,128)S(1)}, f32[64,128]{1,0:T(8,128)S(1)}, u32[]{:S(2)}, u32[]{:S(2)}) %collective-permute-start) | collective-permute-done | bytes 32800 | tf_op jit(solution)/shard_map/ppermute | solution.py:458
  8.4 0.7 %spread.1 = f32[8,32,128]{2,1,0:T(8,128)} custom-call(f32[64,128]{1,0:T(8,128)S(1)} %get-tuple-element.8.mine, f32[64,128]{1,0:T(8,128)S(1)} %collective-permute-done.got), custom_call_target="tpu_custom_call" | custom-call | tf_op jit(solution)/shard_map/spread/pallas_call | solution.py:286
  9.1 7.3 %all-to-all-start = ((f32[8,32,128]{2,1,0:T(8,128)}), f32[8,32,128]{2,1,0:T(8,128)S(1)}, u32[]{:S(2)}, u32[]{:S(2)}) async-start(f32[8,32,128]{2,1,0:T(8,128)} %spread.1), calls=%async_computation | async-start | bytes 262144 | tf_op jit(solution)/shard_map/all_to_all | solution.py:460
  17.1 0.6 %band_weights.1 = (f32[128,128]{1,0:T(8,128)S(1)}, f32[128,128]{1,0:T(8,128)S(1)}) custom-call(s32[1,1]{1,0:T(1,128)S(6)} %copy.9.live.refs_0_, s32[1,4096]{1,0:T(1,128)S(1)} %bitcast.12, f32[1,4096]{1,0:T(1,128)S(1)} %bitcast.15, s32[32,4096]{1,0:T(8,128)S(1)} %copy-done), custom_call_target="tpu_custom_call" | custom-call | flops 600000000 | bytes 700000 | tf_op jit(solution)/shard_map/band_weights/pallas_call | solution.py:266
  17.7 1.0 %collective-permute-start.1 = (f32[128,128]{1,0:T(8,128)S(1)}, f32[128,128]{1,0:T(8,128)S(1)}, u32[]{:S(2)}, u32[]{:S(2)}) collective-permute-start(f32[128,128]{1,0:T(8,128)S(1)} %get-tuple-element.11), channel_id=1, source_target_pairs={{0,1},{1,0},{2,3},{3,2},{4,5},{5,4},{6,7},{7,6},{8,9},{9,8},{10,11... | collective-permute-start | bytes 196616 | tf_op jit(solution)/shard_map/ppermute | solution.py:462
  18.7 0.9 %collective-permute-done.1 = f32[128,128]{1,0:T(8,128)S(1)} collective-permute-done((f32[128,128]{1,0:T(8,128)S(1)}, f32[128,128]{1,0:T(8,128)S(1)}, u32[]{:S(2)}, u32[]{:S(2)}) %collective-permute-start.1) | collective-permute-done | bytes 65568 | tf_op jit(solution)/shard_map/ppermute | solution.py:462
  19.6 1.6 %all-to-all-done.parts = f32[8,32,128]{2,1,0:T(8,128)S(1)} async-done(((f32[8,32,128]{2,1,0:T(8,128)}), f32[8,32,128]{2,1,0:T(8,128)S(1)}, u32[]{:S(2)}, u32[]{:S(2)}) %all-to-all-start) | async-done | bytes 131104 | tf_op jit(solution)/shard_map/all_to_all | solution.py:460
  21.3 14.4 %all_to_all.15.near = f32[16,40,128]{2,1,0:T(8,128)S(1)} all-to-all(f32[16,40,128]{2,1,0:T(8,128)S(1)} %get-tuple-element.12), channel_id=1, replica_groups=mesh['sector'=16,'obl'=16] {'sector'}, dimensions={0} | all-to-all | bytes 655360 | tf_op jit(solution)/shard_map/all_to_all | solution.py:466
  35.8 2.1 %collective-permute-start.2 = (f32[16,32,128]{2,1,0:T(8,128)S(1)}, f32[16,32,128]{2,1,0:T(8,128)S(1)}, u32[]{:S(2)}, u32[]{:S(2)}) collective-permute-start(f32[16,32,128]{2,1,0:T(8,128)S(1)} %slice.4.refs_1_), channel_id=1, source_target_pairs={{0,2},{1,3},{2,0},{3,1},{4,6},{5,7},{6,4},{7,5},{8,10},{9,11},{10,... | collective-permute-start | bytes 786440 | tf_op jit(solution)/shard_map/ppermute | solution.py:468
  37.9 2.5 %collective-permute-start.4 = (f32[16,32,128]{2,1,0:T(8,128)S(1)}, f32[16,32,128]{2,1,0:T(8,128)S(1)}, u32[]{:S(2)}, u32[]{:S(2)}) collective-permute-start(f32[16,32,128]{2,1,0:T(8,128)S(1)} %slice.4.refs_1_), channel_id=1, source_target_pairs={{0,1},{1,0},{2,3},{3,2},{4,5},{5,4},{6,7},{7,6},{8,9},{9,8},{10,11... | collective-permute-start | bytes 786440 | tf_op jit(solution)/shard_map/ppermute | solution.py:469
  40.4 0.0 collective-permute-start.5
  40.5 3.0 %collective-permute-done.5.across = f32[32,128]{1,0:T(8,128)S(1)} collective-permute-done((f32[32,128]{1,0:T(8,128)S(1)}, f32[32,128]{1,0:T(8,128)S(1)}, u32[]{:S(2)}, u32[]{:S(2)}) %collective-permute-start.5) | collective-permute-done | bytes 16416 | tf_op jit(solution)/shard_map/ppermute | solution.py:465
  43.5 0.1 share.1
  43.6 14.1 %all_to_all.16.shares = f32[16,1,128]{2,1,0:T(1,128)S(1)} all-to-all(f32[16,1,128]{2,1,0:T(1,128)S(1)} %share.1), channel_id=1, replica_groups=mesh['sector'=16,'obl'=16] {'obl'}, dimensions={0} | all-to-all | bytes 16384 | tf_op jit(solution)/shard_map/all_to_all | solution.py:471
  57.7 0.6 %total.1 = f32[2,8]{1,0:T(2,128)} custom-call(f32[16,1,128]{2,1,0:T(1,128)S(1)} %all_to_all.16.shares), custom_call_target="tpu_custom_call" | custom-call | tf_op jit(solution)/shard_map/total/pallas_call | solution.py:436
  58.3 0.0 collective-permute-done.2.refs_1_
  58.3 0.7 %collective-permute-start.3 = (f32[16,32,128]{2,1,0:T(8,128)S(1)}, f32[16,32,128]{2,1,0:T(8,128)S(1)}, u32[]{:S(2)}, u32[]{:S(2)}) collective-permute-start(f32[16,32,128]{2,1,0:T(8,128)S(1)} %collective-permute-done.2.refs_1_), channel_id=1, source_target_pairs={{0,1},{1,0},{2,3},{3,2},{4,5},{5,4},{6,7},{7,6},{8,9},{9,8},{10,11... | collective-permute-start | bytes 786440 | tf_op jit(solution)/shard_map/ppermute | solution.py:473
  59.0 0.0 collective-permute-done.4.refs_2_
  59.0 0.8 %lookup_first.1.refs_6_ = f32[8,4096]{1,0:T(8,128)S(1)} custom-call(s32[1,1]{1,0:T(1,128)S(6)} %copy.9.live.refs_0_, f32[16,32,128]{2,1,0:T(8,128)S(1)} %slice.4.refs_1_, f32[16,32,128]{2,1,0:T(8,128)S(1)} %collective-permute-done.4.refs_2_, s32[1,4096]{1,0:T(1,128)S(1)} %bitcast.13, s32[32,4096]{1,0:T(8,128)S(1)} %copy-done), custom_call_target="tpu_custom_call" | custom-call | flops 4300000256 | bytes 1000000 | tf_op jit(solution)/shard_map/lookup_first/pallas_call | solution.py:384
  59.8 0.3 collective-permute-done.3.refs_2_
  60.2 1.5 %lookup_last.1 = f32[8,4096]{1,0:T(8,128)} custom-call(s32[1,1]{1,0:T(1,128)S(6)} %copy.9.live.refs_0_, f32[16,32,128]{2,1,0:T(8,128)S(1)} %collective-permute-done.2.refs_1_, f32[16,32,128]{2,1,0:T(8,128)S(1)} %collective-permute-done.3.refs_2_, s32[1,4096]{1,0:T(1,128)S(1)} %bitcast.14, f32[1,4096]{1,0:T(1,128)S(1)} %bitcast.16, s32[32,4096]{1,0:T(8,128)S(1)} %copy-done, ...), custom_call_target="tpu_custom_call" | custom-call | flops 4300000256 | bytes 1000000 | tf_op jit(solution)/shard_map/lookup_last/pallas_call | solution.py:384
  (7 shorter events, 0.1 us)
Async XLA Ops:
  0.6 16.4 %copy-start = (s32[32,4096]{1,0:T(8,128)S(1)}, s32[32,4096]{1,0:T(8,128)}, u32[]{:S(2)}) copy-start(s32[32,4096]{1,0:T(8,128)} %refs_5_.1) | copy-start | bytes 1572868
  4.2 4.1 %collective-permute-start = (f32[64,128]{1,0:T(8,128)S(1)}, f32[64,128]{1,0:T(8,128)S(1)}, u32[]{:S(2)}, u32[]{:S(2)}) collective-permute-start(f32[64,128]{1,0:T(8,128)S(1)} %get-tuple-element.9), channel_id=1, source_target_pairs={{0,1},{1,0},{2,3},{3,2},{4,5},{5,4},{6,7},{7,6},{8,9},{9,8},{10,11... | collective-permute-start | bytes 98312 | tf_op jit(solution)/shard_map/ppermute | solution.py:458
  9.0 8.0 %copy-start.1 = (s32[4096]{0:T(1024)S(1)}, s32[4096]{0:T(1024)}, u32[]{:S(2)}) copy-start(s32[4096]{0:T(1024)} %param.8) | copy-start | bytes 49156
  9.0 8.0 %copy-start.2 = (f32[4096]{0:T(1024)S(1)}, f32[4096]{0:T(1024)}, u32[]{:S(2)}) copy-start(f32[4096]{0:T(1024)} %param.9) | copy-start | bytes 49156
  9.1 12.2 %all-to-all-start = ((f32[8,32,128]{2,1,0:T(8,128)}), f32[8,32,128]{2,1,0:T(8,128)S(1)}, u32[]{:S(2)}, u32[]{:S(2)}) async-start(f32[8,32,128]{2,1,0:T(8,128)} %spread.1), calls=%async_computation | async-start | bytes 262144 | tf_op jit(solution)/shard_map/all_to_all | solution.py:460
  17.7 1.9 %collective-permute-start.1 = (f32[128,128]{1,0:T(8,128)S(1)}, f32[128,128]{1,0:T(8,128)S(1)}, u32[]{:S(2)}, u32[]{:S(2)}) collective-permute-start(f32[128,128]{1,0:T(8,128)S(1)} %get-tuple-element.11), channel_id=1, source_target_pairs={{0,1},{1,0},{2,3},{3,2},{4,5},{5,4},{6,7},{7,6},{8,9},{9,8},{10,11... | collective-permute-start | bytes 196616 | tf_op jit(solution)/shard_map/ppermute | solution.py:462
  35.8 22.5 %collective-permute-start.2 = (f32[16,32,128]{2,1,0:T(8,128)S(1)}, f32[16,32,128]{2,1,0:T(8,128)S(1)}, u32[]{:S(2)}, u32[]{:S(2)}) collective-permute-start(f32[16,32,128]{2,1,0:T(8,128)S(1)} %slice.4.refs_1_), channel_id=1, source_target_pairs={{0,2},{1,3},{2,0},{3,1},{4,6},{5,7},{6,4},{7,5},{8,10},{9,11},{10,... | collective-permute-start | bytes 786440 | tf_op jit(solution)/shard_map/ppermute | solution.py:468
  37.9 21.1 %collective-permute-start.4 = (f32[16,32,128]{2,1,0:T(8,128)S(1)}, f32[16,32,128]{2,1,0:T(8,128)S(1)}, u32[]{:S(2)}, u32[]{:S(2)}) collective-permute-start(f32[16,32,128]{2,1,0:T(8,128)S(1)} %slice.4.refs_1_), channel_id=1, source_target_pairs={{0,1},{1,0},{2,3},{3,2},{4,5},{5,4},{6,7},{7,6},{8,9},{9,8},{10,11... | collective-permute-start | bytes 786440 | tf_op jit(solution)/shard_map/ppermute | solution.py:469
  40.4 3.1 %collective-permute-start.5 = (f32[32,128]{1,0:T(8,128)S(1)}, f32[32,128]{1,0:T(8,128)S(1)}, u32[]{:S(2)}, u32[]{:S(2)}) collective-permute-start(f32[32,128]{1,0:T(8,128)S(1)} %get-tuple-element.13.own), channel_id=1, source_target_pairs={{0,2},{1,3},{2,0},{3,1},{4,6},{5,7},{6,4},{7,5},{8,10},{9,11},{10,... | collective-permute-start | bytes 49160 | tf_op jit(solution)/shard_map/ppermute | solution.py:465
  58.3 1.8 %collective-permute-start.3 = (f32[16,32,128]{2,1,0:T(8,128)S(1)}, f32[16,32,128]{2,1,0:T(8,128)S(1)}, u32[]{:S(2)}, u32[]{:S(2)}) collective-permute-start(f32[16,32,128]{2,1,0:T(8,128)S(1)} %collective-permute-done.2.refs_1_), channel_id=1, source_target_pairs={{0,1},{1,0},{2,3},{3,2},{4,5},{5,4},{6,7},{7,6},{8,9},{9,8},{10,11... | collective-permute-start | bytes 786440 | tf_op jit(solution)/shard_map/ppermute | solution.py:473
